TPU v7x, 256 devices: a whole 4x4x8 slice. The times are simulated.
256 devices in a mesh: seq: 32 (over y, z), tp: 8 (over x, core).
Axes of the slice: x: 4, y: 4, z: 8, core: 2. Of those that a mesh axis runs over, the one named last changes fastest.
Arguments:
- tokens: bfloat16 [16384, 2560], P('seq', 'tp'), may hold values from -6 to 6
- gate_weight: bfloat16 [2560, 5120], P(None, 'tp'), may hold values from -0.125 to 0.125
- inner_weight: bfloat16 [2560, 5120], P(None, 'tp'), may hold values from -0.125 to 0.125
- state_weight: bfloat16 [2560, 256], replicated, may hold values from -0.125 to 0.125
- step_weight: bfloat16 [2560, 80], P(None, 'tp'), may hold values from -0.125 to 0.125
- conv_inner: float32 [4, 5120], P(None, 'tp'), may hold values from -3 to 3
- conv_state: float32 [4, 256], replicated, may hold values from -3 to 3
- step_bias: float32 [80], P('tp'), may hold values from -3 to 1
- decay_rate: float32 [80], P('tp'), may hold values from 1e-05 to 0.02
- skip_gain: float32 [80], P('tp'), may hold values from 0.5 to 2
- norm_gain: float32 [5120], P('tp'), may hold values from 0.1 to 1.9
- out_weight: bfloat16 [5120, 2560], P('tp'), may hold values from -0.078125 to 0.078125
Outputs:
- layer_out: bfloat16 [16384, 2560], P(('seq', 'tp'))
All inputs are finite; a program needn't handle non-finite values.
Results may differ from a plain program's by a relative error of at most 0.018.
Values may be sent and summed in bfloat16 or wider, within the bound.
A program may use at most 128 MiB of HBM per device.

v0:
```python
import jax
import jax.numpy as jnp
from jax import lax
from jax.sharding import Mesh
from jax.sharding import PartitionSpec as P

GROUP = 256
SEQ = ("seq_0", "seq_1")
SEQ_TP = ("seq_0", "seq_1", "tp")


def filled_with(shard, identity):
    return jax.tree.map(
        lambda a, e: jnp.broadcast_to(jnp.asarray(e, a.dtype), a.shape), shard, identity
    )


def carried_in(shard, axes, combine, identity):
    before = start = filled_with(shard, identity)
    total = shard
    for axis in reversed(axes):
        size, place = (lax.axis_size(axis), lax.axis_index(axis))
        pieces = jax.tree.map(
            lambda part, kind: lax.all_gather(part.astype(kind), axis),
            total,
            (jnp.bfloat16, jnp.bfloat16),
        )
        inside, total = (start, start)
        for k in range(size):
            passed = k < place
            total = combine(
                total, jax.tree.map(lambda part, own: part[k].astype(own.dtype), pieces, shard)
            )
            inside = jax.tree.map(lambda new, old: jnp.where(passed, new, old), total, inside)
        before = combine(inside, before)
    return before


def laid_out(pieces, dim):
    pieces = jnp.moveaxis(pieces, 0, dim)
    dims = pieces.shape
    return pieces.reshape(*dims[:dim], dims[dim] * dims[dim + 1], *dims[dim + 2 :])


def from_everyone(shard, axis):
    size = lax.axis_size(axis)
    return lax.all_to_all(
        jnp.broadcast_to(shard[None], (size, *shard.shape)), axis, 0, 0, tiled=True
    )


def collect(shard, axis, dim):
    return laid_out(from_everyone(shard, axis), dim)


def passed_along(shard, axis, by):
    size = lax.axis_size(axis)
    pairs = [(i, i + by) for i in range(size) if 0 <= i + by < size]
    return lax.ppermute(shard, axis, pairs)


def over_copies(shard, axis):
    everything = from_everyone(shard, axis)
    return jnp.sum(everything, axis=0)


def group_decay(inner_blk, inject_blk, step_blk, log_blk):
    cumulative = jnp.cumsum(log_blk, axis=0)
    ending = cumulative[-1]
    tail_weight = jnp.exp(ending[None, :] - cumulative) * step_blk
    scaled = inner_blk.astype(jnp.float32) * tail_weight[:, :, None]
    contribution = jnp.einsum("thp,tn->hpn", scaled, inject_blk.astype(jnp.float32))
    return (cumulative, ending, contribution)


def group_intra(inner_blk, inject_blk, readout_blk, step_blk, cumulative):
    scores = jnp.dot(readout_blk, inject_blk.T, preferred_element_type=jnp.float32)
    length = scores.shape[0]
    causal = jnp.arange(length)[:, None] >= jnp.arange(length)[None, :]
    log_gaps = cumulative.T[:, :, None] - cumulative.T[:, None, :]
    decay_mask = jnp.exp(jnp.where(causal[None], log_gaps, -jnp.inf))
    mixing = (scores[None] * decay_mask * step_blk.T[:, None, :]).astype(jnp.bfloat16)
    return jnp.einsum("hts,shp->thp", mixing, inner_blk, preferred_element_type=jnp.float32)


def read_state(readout_blk, cumulative, carried):
    reads = jnp.einsum("tn,hpn->thp", readout_blk.astype(jnp.float32), carried)
    return reads * jnp.exp(cumulative)[:, :, None]


def combine(earlier, later):
    return (earlier[0] + later[0], jnp.exp(later[0])[:, None, None] * earlier[1] + later[1])


def receive(decay_total, local_state):
    zero_state = jnp.zeros_like(local_state)
    scanned = carried_in(
        (decay_total, local_state), SEQ, combine, (jnp.zeros_like(decay_total), zero_state)
    )
    return scanned[1]


def on_device(
    tokens,
    gate_weight,
    inner_weight,
    state_weight,
    step_weight,
    conv_inner,
    conv_state,
    step_bias,
    decay_rate,
    skip_gain,
    norm_gain,
    out_weight,
):
    tok_rows = tokens.shape[0]
    weights = (gate_weight, inner_weight, state_weight, step_weight)
    segment = collect(tokens, "tp", 1)
    gate_raw, inner_raw, state_raw, step_raw = tuple(
        (jnp.dot(segment, weight, preferred_element_type=jnp.float32) for weight in weights)
    )
    gate_act = gate_raw.astype(jnp.bfloat16)
    mixed_in = jnp.concatenate([inner_raw, state_raw], axis=1).astype(jnp.bfloat16)
    taps = conv_inner.shape[0]
    edge_rows = passed_along(mixed_in[tok_rows - (taps - 1) :], SEQ, 1)
    padded = jnp.concatenate([edge_rows, mixed_in], axis=0)
    kernel = jnp.concatenate([conv_inner, conv_state], axis=1)
    conv_sum = jnp.zeros(mixed_in.shape, jnp.float32)
    for tap in range(taps):
        conv_sum = (
            conv_sum + padded[tap : tap + tok_rows].astype(jnp.float32) * kernel[tap][None, :]
        )
    conv_out = jax.nn.silu(conv_sum).astype(jnp.bfloat16)
    width_inner = inner_weight.shape[1]
    head_count = step_weight.shape[1]
    head_width = width_inner // head_count
    state_size = state_weight.shape[1] // 2
    inner_act = conv_out[:, :width_inner].reshape(tok_rows, head_count, head_width)
    inject = conv_out[:, width_inner : width_inner + state_size]
    readout = conv_out[:, width_inner + state_size :]
    time_step = jax.nn.softplus(step_raw + step_bias[None, :])
    log_decay = -time_step * decay_rate[None, :]
    block_count = tok_rows // GROUP
    pieces = []
    for group_number in range(block_count):
        row_span = slice(group_number * GROUP, (group_number + 1) * GROUP)
        pieces.append(
            (
                inner_act[row_span],
                inject[row_span],
                readout[row_span],
                time_step[row_span],
                log_decay[row_span],
            )
        )
    outputs = []
    carried = jnp.zeros((head_count, head_width, state_size), jnp.float32)
    decay_total = jnp.zeros((head_count,), jnp.float32)
    summaries = []
    for group_number in range(block_count):
        inner_blk, inject_blk, readout_blk, step_blk, log_blk = pieces[group_number]
        cumulative, ending, contribution = group_decay(inner_blk, inject_blk, step_blk, log_blk)
        block_out = group_intra(inner_blk, inject_blk, readout_blk, step_blk, cumulative)
        if group_number > 0:
            block_out = block_out + read_state(readout_blk, cumulative, carried)
        outputs.append(block_out)
        carried = jnp.exp(ending)[:, None, None] * carried + contribution
        decay_total = decay_total + ending
        summaries.append((cumulative, ending))
    incoming = receive(decay_total, carried)
    offset = jnp.zeros((head_count,), jnp.float32)
    for group_number in range(block_count):
        cumulative, ending = summaries[group_number]
        outputs[group_number] = outputs[group_number] + read_state(
            pieces[group_number][2], cumulative + offset[None, :], incoming
        )
        offset = offset + ending
    ssd_out = jnp.concatenate(outputs, axis=0) + skip_gain[None, :, None] * inner_act.astype(
        jnp.float32
    )
    gated = ssd_out.reshape(tok_rows, width_inner) * jax.nn.silu(gate_act.astype(jnp.float32))
    square_total = over_copies(jnp.sum(gated * gated, axis=1), "tp")
    mean_square = square_total / (width_inner * lax.axis_size("tp"))
    normed = (gated * lax.rsqrt(mean_square + 1e-05)[:, None] * norm_gain[None, :]).astype(
        jnp.bfloat16
    )
    return lax.psum_scatter(
        jnp.dot(normed, out_weight, preferred_element_type=jnp.float32).astype(jnp.bfloat16),
        "tp",
        scatter_dimension=0,
        tiled=True,
    )


def solution(mesh):
    split = Mesh(mesh.devices.reshape(4, 8, mesh.shape["tp"]), ("seq_0", "seq_1", "tp"))
    return jax.shard_map(
        on_device,
        mesh=split,
        in_specs=(
            P(SEQ, "tp"),
            P(None, "tp"),
            P(None, "tp"),
            P(),
            P(None, "tp"),
            P(None, "tp"),
            P(),
            P("tp"),
            P("tp"),
            P("tp"),
            P("tp"),
            P("tp", None),
        ),
        out_specs=P(SEQ_TP, None),
        check_vma=False,
    )
```

profile of v0, /device:TPU:1, one launch (start us, length us, event | category | flops | bytes accessed | tf_op | source)
XLA Modules:
  0.0 205.4 jit_solution(18416952025437515956)
XLA Ops:
  6.5 2.9 %broadcast_in_dim.22 = bf16[8,512,320]{1,2,0:T(8,128)(2,1)} broadcast(bf16[512,320]{0,1:T(8,128)(2,1)} %param.12), dimensions={1,2} | broadcast | bytes 2949120 | tf_op jit(solution)/shard_map/broadcast_in_dim | solution.py:48
  9.4 7.6 %all-to-all-start = ((bf16[8,512,320]{1,2,0:T(8,128)(2,1)}), bf16[8,512,320]{1,2,0:T(8,128)(2,1)}, u32[]{:S(2)}, u32[]{:S(2)}) async-start(bf16[8,512,320]{1,2,0:T(8,128)(2,1)} %broadcast_in_dim.22), calls=%async_computation | async-start | bytes 5242880 | tf_op jit(solution)/shard_map/all_to_all | solution.py:47
  17.1 31.9 %all-to-all-done = bf16[8,512,320]{1,2,0:T(8,128)(2,1)} async-done(((bf16[8,512,320]{1,2,0:T(8,128)(2,1)}), bf16[8,512,320]{1,2,0:T(8,128)(2,1)}, u32[]{:S(2)}, u32[]{:S(2)}) %all-to-all-start) | async-done | bytes 2621472 | tf_op jit(solution)/shard_map/all_to_all | solution.py:47
  49.0 2.2 %negate_multiply_fusion = (f32[512,10]{0,1:T(8,128)S(1)}, f32[512,10]{0,1:T(8,128)S(1)}) fusion(f32[10]{0:T(128)S(1)} %copy-done.14, f32[10]{0:T(128)S(1)} %copy-done.15, bf16[512,2560]{0,1:T(8,128)(2,1)} %bitcast.1, bf16[2560,10]{0,1:T(8,128)(2,1)S(1)} %copy-done.7), kind=kOutput, calls=%fused_computation.128 | convolution fusion | flops 26260480 | bytes 2713680 | tf_op jit(solution)/shard_map/dot_general | solution.py:121
  51.3 0.6 reduce-window.16
  51.9 0.2 slice_reduce_fusion
  52.1 0.1 broadcast_add_fusion
  52.2 0.6 reduce-window.14
  52.8 0.2 slice_reduce_fusion.1
  53.0 0.1 broadcast_add_fusion.1
  53.1 5.1 %convolution_convert_fusion.2 = bf16[512,640]{1,0:T(8,128)(2,1)S(1)} fusion(bf16[512,2560]{0,1:T(8,128)(2,1)} %bitcast.1, bf16[2560,640]{1,0:T(8,128)(2,1)} %param.14), kind=kOutput, calls=%fused_computation.7 | convolution fusion | flops 1678049280 | bytes 6553600 | tf_op jit(solution)/shard_map/dot_general | solution.py:121
  58.2 2.6 %convolution_convert_fusion.3 = bf16[512,256]{1,0:T(8,128)(2,1)S(1)} fusion(bf16[512,2560]{0,1:T(8,128)(2,1)} %bitcast.1, bf16[2560,256]{1,0:T(8,128)(2,1)S(1)} %copy-done.4), kind=kOutput, calls=%fused_computation.37 | convolution fusion | flops 671219712 | bytes 4194304 | tf_op jit(solution)/shard_map/dot_general | solution.py:121
  60.8 1.8 collective-permute-start
  62.7 0.2 slice_reduce_fusion.2
  62.9 0.6 slice_bitcast_fusion.7
  63.5 0.2 maximum_maximum_fusion
  63.8 1.1 multiply_convert_fusion.2
  64.9 0.9 copy-done.2
  65.8 0.9 fusion.109
  66.7 1.9 copy.53
  68.6 1.9 copy.58
  70.5 1.2 convolution_add_fusion.1
  71.8 0.7 copy-done.3
  72.5 1.9 fusion.23
  74.5 0.7 mul.418
  75.2 0.7 iota_compare_fusion
  75.9 0.2 fusion.81
  76.0 15.4 %all-gather.1 = bf16[8,1,10]{2,1,0:T(2,128)(2,1)S(1)} all-gather(bf16[1,1,10]{2,1,0:T(2,128)(2,1)S(1)} %bitcast.286), channel_id=1, replica_groups=mesh['seq_0'=4,'seq_1'=8,'tp'=8] {'seq_1'}, dimensions={0}, use_global_device_ids=true | all-gather | bytes 180 | tf_op jit(solution)/shard_map/all_gather | solution.py:24
  91.4 0.5 fusion.83
  92.0 8.0 %all-gather.2 = bf16[4,1,10]{2,1,0:T(2,128)(2,1)S(1)} all-gather(bf16[1,1,10]{2,1,0:T(2,128)(2,1)S(1)} %get-tuple-element.24), channel_id=1, replica_groups=mesh['seq_0'=4,'seq_1'=8,'tp'=8] {'seq_0'}, dimensions={0}, use_global_device_ids=true | all-gather | bytes 100 | tf_op jit(solution)/shard_map/all_gather | solution.py:24
  99.9 0.6 fusion.93
  100.5 1.8 fusion.73
  102.3 1.8 fusion.69
  104.0 2.1 %convolution_multiply_fusion.1 = f32[256,10,64]{0,2,1:T(8,128)} fusion(f32[10,64,128]{2,1,0:T(8,128)} %copy-done.3, f32[256,10]{0,1:T(8,128)S(1)} %get-tuple-element.22, bf16[512,896]{1,0:T(8,128)(2,1)} %copy-done.2), kind=kOutput, calls=%fused_computation.35 | convolution fusion | flops 42106880 | bytes 1058816 | tf_op jit(solution)/shard_map/tn,hpn->thp/dot_general | solution.py:87
  106.2 6.2 %all-gather.5.cloned.1.call-done = bf16[80,64,128]{2,1,0:T(8,128)(2,1)} async-done(((bf16[10,64,128]{2,1,0:T(8,128)(2,1)}), bf16[80,64,128]{2,1,0:T(8,128)(2,1)}) %all-gather.5.cloned.1.call-update) | async-done | bytes 1310736 | tf_op jit(solution)/shard_map/all_gather | solution.py:24
  112.3 1.8 fusion.63
  114.2 11.0 %all_gather.22 = bf16[4,10,64,128]{3,2,1,0:T(8,128)(2,1)S(1)} all-gather(bf16[1,10,64,128]{3,2,1,0:T(8,128)(2,1)S(1)} %fusion.63), channel_id=1, replica_groups=mesh['seq_0'=4,'seq_1'=8,'tp'=8] {'seq_0'}, dimensions={0}, use_global_device_ids=true | all-gather | bytes 819200 | tf_op jit(solution)/shard_map/all_gather | solution.py:24
  125.2 1.6 fusion.39
  126.8 1.1 convolution_multiply_fusion.2
  128.0 1.7 fusion.21
  129.7 2.2 %copy.59 = f32[256,640]{1,0:T(8,128)} copy(f32[256,640]{0,1:T(8,128)} %bitcast.275) | data formatting | bytes 1310720 | tf_op jit(solution)/shard_map/concatenate | solution.py:179
  131.9 1.1 convolution_multiply_fusion
  133.0 3.0 %fusion.22 = f32[256,10,64]{0,2,1:T(8,128)} fusion(f32[256,10,64]{0,2,1:T(8,128)S(1)} %convolution_multiply_fusion, f32[256,10,64]{0,2,1:T(8,128)} %convolution_multiply_fusion.1, bf16[256,10,64]{0,2,1:T(8,128)(2,1)} %bitcast.271, f32[10,256]{1,0:T(8,128)S(1)} %copy-done.10, f32[10,256]{1,0:T(8,128)S(1)} %bitcast.279, f32[256,256]{1,0:T(8,128)} %fusion.69, ...), kind=kOutput, calls=%fused_computation.33 | convolution fusion | flops 87490560 | bytes 2641920 | tf_op jit(solution)/shard_map/hts,shp->thp/dot_general | solution.py:83
  136.0 2.2 %copy.60 = f32[256,640]{1,0:T(8,128)} copy(f32[256,640]{0,1:T(8,128)} %bitcast.274) | data formatting | bytes 1310720 | tf_op jit(solution)/shard_map/concatenate | solution.py:179
  138.2 6.8 %multiply_reduce_fusion = (f32[512]{0:T(512)S(1)}, f32[512,640]{1,0:T(8,128)}) fusion(bf16[512,896]{1,0:T(8,128)(2,1)} %copy-done.2, f32[640]{0:T(1024)S(1)} %copy-done.12, f32[256,640]{1,0:T(8,128)} %copy.60, f32[256,640]{1,0:T(8,128)} %copy.59, bf16[512,2560]{0,1:T(8,128)(2,1)} %bitcast.1, bf16[2560,640]{1,0:T(8,128)(2,1)} %param.13), kind=kOutput, calls=%fused_computation.16 | convolution fusion | flops 1681980928 | bytes 9179648 | tf_op jit(solution)/shard_map/dot_general | solution.py:121
  145.0 17.1 %all_to_all.11 = f32[8,1,512]{2,1,0:T(1,128)S(1)} all-to-all(f32[8,1,512]{2,1,0:T(1,128)S(1)} %broadcast_in_dim.25), channel_id=1, replica_groups=mesh['seq_0'=4,'seq_1'=8,'tp'=8] {'tp'}, dimensions={0} | all-to-all | bytes 32768 | tf_op jit(solution)/shard_map/all_to_all | solution.py:47
  162.1 5.1 %convolution_convert_fusion = bf16[512,2560]{1,0:T(8,128)(2,1)} fusion(bf16[640,2560]{1,0:T(8,128)(2,1)S(1)} %copy-done, f32[512,640]{1,0:T(8,128)} %get-tuple-element.10, f32[640]{0:T(1024)S(1)} %copy-done.17, f32[512]{0:T(512)S(1)} %add_rsqrt_fusion), kind=kOutput, calls=%fused_computation | convolution fusion | flops 1680015360 | bytes 7213568 | tf_op jit(solution)/shard_map/dot_general | solution.py:189
  167.3 31.3 %reduce-scatter.2.cloned.1.call-done = bf16[64,2560]{1,0:T(8,128)(2,1)} async-done(((bf16[512,2560]{1,0:T(8,128)(2,1)}), bf16[64,2560]{1,0:T(8,128)(2,1)}) %reduce-scatter.2.cloned.1.call-update) | async-done | bytes 327696 | tf_op jit(solution)/shard_map/reduce_scatter | solution.py:188
  (66 shorter events, 0.5 us)
Async XLA Ops:
  6.5 155.6 %copy-start = (bf16[640,2560]{1,0:T(8,128)(2,1)S(1)}, bf16[640,2560]{1,0:T(8,128)(2,1)}, u32[]{:S(2)}) copy-start(bf16[640,2560]{1,0:T(8,128)(2,1)} %param.23) | copy-start | bytes 9830404
  9.4 7.6 %copy-start.11 = (f32[4,640]{1,0:T(4,128)S(1)}, f32[4,640]{1,0:T(4,128)}, u32[]{:S(2)}) copy-start(f32[4,640]{1,0:T(4,128)} %param.17) | copy-start | bytes 30724
  9.4 7.6 %copy-start.13 = (f32[4,256]{1,0:T(4,128)S(1)}, f32[4,256]{1,0:T(4,128)}, u32[]{:S(2)}) copy-start(f32[4,256]{1,0:T(4,128)} %param.18) | copy-start | bytes 12292
  9.4 39.6 %copy-start.7 = (bf16[2560,10]{0,1:T(8,128)(2,1)S(1)}, bf16[2560,10]{0,1:T(8,128)(2,1)}, u32[]{:S(2)}) copy-start(bf16[2560,10]{0,1:T(8,128)(2,1)} %param.16) | copy-start | bytes 153604
  9.4 39.6 %copy-start.14 = (f32[10]{0:T(128)S(1)}, f32[10]{0:T(128)}, u32[]{:S(2)}) copy-start(f32[10]{0:T(128)} %param.20) | copy-start | bytes 124
  9.4 39.6 %copy-start.15 = (f32[10]{0:T(128)S(1)}, f32[10]{0:T(128)}, u32[]{:S(2)}) copy-start(f32[10]{0:T(128)} %param.19) | copy-start | bytes 124
  9.4 39.6 %all-to-all-start = ((bf16[8,512,320]{1,2,0:T(8,128)(2,1)}), bf16[8,512,320]{1,2,0:T(8,128)(2,1)}, u32[]{:S(2)}, u32[]{:S(2)}) async-start(bf16[8,512,320]{1,2,0:T(8,128)(2,1)} %broadcast_in_dim.22), calls=%async_computation | async-start | bytes 5242880 | tf_op jit(solution)/shard_map/all_to_all | solution.py:47
  17.0 95.3 %all-gather.5.cloned.1.call-start = ((), (), s32[]{:S(2)}) async-start(), calls=%async_computation.4 | async-start | bytes 1474560 | tf_op jit(solution)/shard_map/all_gather | solution.py:24
  53.1 5.1 %copy-start.4 = (bf16[2560,256]{1,0:T(8,128)(2,1)S(1)}, bf16[2560,256]{1,0:T(8,128)(2,1)}, u32[]{:S(2)}) copy-start(bf16[2560,256]{1,0:T(8,128)(2,1)} %param.15) | copy-start | bytes 3932164
  60.8 2.7 %collective-permute-start = (bf16[3,896]{1,0:T(4,128)(2,1)S(1)}, bf16[3,896]{1,0:T(4,128)(2,1)S(1)}, u32[]{:S(2)}, u32[]{:S(2)}) collective-permute-start(bf16[3,896]{1,0:T(4,128)(2,1)S(1)} %fusion.80), channel_id=1, source_target_pairs={{0,8},{8,16},{16,24},{24,32},{32,40},{40,48},{48,56},{56,64},{64,7... | collective-permute-start | bytes 16136 | tf_op jit(solution)/shard_map/ppermute | solution.py:59
  64.9 0.9 copy-start.2
  66.7 7.7 %copy-start.16 = (f32[10]{0:T(128)S(1)}, f32[10]{0:T(128)}, u32[]{:S(2)}) copy-start(f32[10]{0:T(128)} %param.21) | copy-start | bytes 124
  71.7 0.7 copy-start.3
  74.4 124.2 %reduce-scatter.2.cloned.1.call-start = ((), (), s32[]{:S(2)}) async-start(), calls=%async_computation.3 | async-start | bytes 2949120 | tf_op jit(solution)/shard_map/reduce_scatter | solution.py:188
  112.3 12.9 %copy-start.1 = (bf16[80,64,128]{2,1,0:T(8,128)(2,1)S(1)}, bf16[80,64,128]{2,1,0:T(8,128)(2,1)}, u32[]{:S(2)}) copy-start(bf16[80,64,128]{2,1,0:T(8,128)(2,1)} %all-gather.5.cloned.1.call-done) | copy-start | bytes 3932164
  114.2 13.8 %copy-start.5 = (bf16[256,640]{0,1:T(8,128)(2,1)S(1)}, bf16[256,640]{0,1:T(8,128)(2,1)}, u32[]{:S(2)}) copy-start(bf16[256,640]{0,1:T(8,128)(2,1)} %copy.53) | copy-start | bytes 983044
  114.2 13.8 %copy-start.6 = (f32[256,256]{1,0:T(8,128)S(1)}, f32[256,256]{1,0:T(8,128)}, u32[]{:S(2)}) copy-start(f32[256,256]{1,0:T(8,128)} %fusion.73) | copy-start | bytes 786436
  114.2 13.8 %copy-start.8 = (pred[256,256]{1,0:T(8,128)(4,1)S(1)}, pred[256,256]{1,0:T(8,128)(4,1)}, u32[]{:S(2)}) copy-start(pred[256,256]{1,0:T(8,128)(4,1)} %iota_compare_fusion) | copy-start | bytes 196612
  129.7 3.3 %copy-start.9 = (pred[256,256]{1,0:T(8,128)(4,1)S(1)}, pred[256,256]{1,0:T(8,128)(4,1)}, u32[]{:S(2)}) copy-start(pred[256,256]{1,0:T(8,128)(4,1)} %iota_compare_fusion) | copy-start | bytes 196612
  129.7 3.3 %copy-start.10 = (f32[10,256]{1,0:T(8,128)S(1)}, f32[10,256]{1,0:T(8,128)}, u32[]{:S(2)}) copy-start(f32[10,256]{1,0:T(8,128)} %get-tuple-element.17) | copy-start | bytes 30724
  133.0 5.2 %copy-start.12 = (f32[640]{0:T(1024)S(1)}, f32[640]{0:T(1024)}, u32[]{:S(2)}) copy-start(f32[640]{0:T(1024)} %mul.418) | copy-start | bytes 7684
  138.2 23.9 %copy-start.17 = (f32[640]{0:T(1024)S(1)}, f32[640]{0:T(1024)}, u32[]{:S(2)}) copy-start(f32[640]{0:T(1024)} %param.22) | copy-start | bytes 7684
Sparse Core Ops, SparseCore 0:
  74.5 37.7 all-gather.4
  167.4 31.1 reduce-scatter.1
where the time goes:
time: 208 us; the launch traced here: 205 us
  waiting for transfers between devices  69.4 us (33%)
  blocking collectives  51.5 us (25%)
  matrix products  37.4 us (18%)
  local copies, waits for them, and re-layouts  15.1 us (7%)
  between operations  13.8 us (7%)
  starting transfers between devices  9.49 us (5%)
  other arithmetic  8.86 us (4%)
    all_gather x3, blocking collectives, carried_in(): lax.all_gather(part.astype(kind), axis)  34.4 us
    all_to_all x1, waiting for transfers between devices, from_everyone(): lax.all_to_all(jnp.broadcast_to(shard[None], (size, *shard.shape)), axis,...  31.9 us
    reduce_scatter x1, waiting for transfers between devices, on_device(): lax.psum_scatter(jnp.dot(normed, out_weight, preferred_element_type=jnp.f...  31.3 us
    all_to_all x1, blocking collectives, from_everyone(): lax.all_to_all(jnp.broadcast_to(shard[None], (size, *shard.shape)), axis,...  17.1 us
    dot_general x4, matrix products, on_device(): jnp.dot(segment, weight, preferred_element_type=jnp.float32)  16.7 us
    all_to_all x1, starting transfers between devices, from_everyone(): lax.all_to_all(jnp.broadcast_to(shard[None], (size, *shard.shape)), axis,...  7.6 us
    all_gather x1, waiting for transfers between devices, carried_in(): lax.all_gather(part.astype(kind), axis)  6.18 us
    dot_general x1, matrix products, on_device(): jnp.dot(normed, out_weight, preferred_element_type=jnp.float32)  5.08 us
  transfers between devices with their start and end apart: 4, of which 3 were waited for; matrix products, arithmetic and copies ran while one was open for 4% of the time, Pallas kernels for 0%

commit v1 on v0

v1 whole, which is shorter than its diff:
```python
import jax
import jax.numpy as jnp
from jax import lax
from jax.experimental import pallas as pl
from jax.experimental.pallas import tpu as pltpu
from jax.sharding import PartitionSpec as P

MESH = pl.DeviceIdType.MESH
F32 = jnp.float32
BF16 = jnp.bfloat16
ROWS = 512
GROUP = 256
KD = 320
D = 2560
CH = 640
HD = 10
ST = 128
CONV = CH + 2 * ST
QC = 640
NQ = D // QC
LOG2E = 1.4426950408889634
INNER = 5120


def split2(v):
    hi = v.astype(BF16)
    return hi, (v - hi.astype(F32)).astype(BF16)


def dot(a, b):
    return jnp.dot(a, b, preferred_element_type=F32)


def dot_nt(a, b):
    return lax.dot_general(a, b, (((1,), (1,)), ((), ())), preferred_element_type=F32)


def silu(v):
    return 0.5 * v * (1.0 + jnp.tanh(0.5 * v))


def kernel(
    tok, w_gate, w_inner, w_state, w_step, k_inner, k_state, bias, rate, skip, gain, w_out,
    out,
    xb, wg, wi, ws, wt, wo,
    acc_i, acc_s, acc_t, acc_g, mx, act, edge_s, edge_r,
    small, expand, cum_s, dt_s, cumt_s, dtt_s,
    ssd, gexp, st_bf, st_f, c0_s, z_recv, t_send, t_recv, pref, y_send, yt_send, y_recv, yt_recv, f_send, inc, carr,
    gated, sq_send, sq_recv, keep, d_send, d_recv, r1_send, r1_recv, r2_send, fin_l, fin_r, scale_s,
    loc_sem, g_send, g_recv, e_sem, zs_sem, zr_sem, ts_sem, tr_sem, ys_sem, yr_sem, yts_sem, ytr_sem, fs_sem, fr_sem,
    qs_sem, qr_sem, ds_sem, dr_sem, rs_sem, rr_sem,
):
    seq = lax.axis_index("seq")
    tp = lax.axis_index("tp")
    x = tp // 2
    c = tp % 2
    y = seq // 8
    z = seq % 8
    partner = 2 * x + (1 - c)
    rx, lx, ox = (x + 1) % 4, (x + 3) % 4, (x + 2) % 4
    right, left, opp = 2 * rx + c, 2 * lx + c, 2 * ox + c
    nxt, prv = (seq + 1) % 32, (seq + 31) % 32

    def remote(src, dst, ssem, rsem, **where):
        return pltpu.make_async_remote_copy(
            src_ref=src, dst_ref=dst, send_sem=ssem, recv_sem=rsem, device_id=where, device_id_type=MESH
        )

    loads = [
        pltpu.make_async_copy(tok, xb.at[tp], loc_sem.at[0]),
        pltpu.make_async_copy(w_inner, wi, loc_sem.at[1]),
        pltpu.make_async_copy(w_state, ws, loc_sem.at[2]),
        pltpu.make_async_copy(w_step, wt, loc_sem.at[3]),
        pltpu.make_async_copy(w_gate, wg, loc_sem.at[4]),
        pltpu.make_async_copy(w_out, wo, loc_sem.at[5]),
    ]
    for load in loads:
        load.start()

    barrier = pltpu.get_barrier_semaphore()
    for k in range(1, 8):
        pl.semaphore_signal(barrier, inc=1, device_id={"tp": (tp + k) % 8}, device_id_type=MESH)
    for k in range(1, 8):
        pl.semaphore_signal(barrier, inc=1, device_id={"seq": y * 8 + (z + k) % 8}, device_id_type=MESH)
    for k in range(1, 4):
        pl.semaphore_signal(barrier, inc=1, device_id={"seq": ((y + k) % 4) * 8 + z}, device_id_type=MESH)
    for s in (nxt, prv):
        pl.semaphore_signal(barrier, inc=1, device_id={"seq": s}, device_id_type=MESH)

    er = lax.broadcasted_iota(jnp.int32, (ST, CH), 0)
    ec = lax.broadcasted_iota(jnp.int32, (ST, CH), 1)
    off = ec - er * 64
    expand[...] = jnp.where((off >= 0) & (off < 64), 1.0, 0.0).astype(BF16)
    small[...] = jnp.zeros_like(small)
    small[0:1, 0:HD] = bias[...]
    small[8:9, 0:HD] = rate[...]
    small[16:17, 0:HD] = skip[...]
    acc_t[...] = jnp.zeros_like(acc_t)

    def expanded(v):
        hi, lo = split2(v)
        return dot(hi, expand[...]) + dot(lo, expand[...])

    loads[0].wait()
    pl.semaphore_wait(barrier, 19)

    def piece(src, half, to, ssem):
        part = xb.at[src, pl.ds(half * GROUP, GROUP), :]
        return remote(part, part, ssem, g_recv.at[src, half], tp=to)

    sent = []

    def send(src, half, to, ssem):
        copy = piece(src, half, to, ssem)
        copy.start()
        sent.append(copy)

    def arrived(src, half):
        piece(src, half, partner, g_send.at[0]).wait_recv()

    send(tp, 0, right, g_send.at[0])
    send(tp, 1, left, g_send.at[1])
    send(tp, 1, right, g_send.at[2])
    send(tp, 0, left, g_send.at[3])
    send(tp, 0, partner, g_send.at[4])
    send(tp, 1, partner, g_send.at[5])
    for load in loads[1:4]:
        load.wait()

    def accumulate(src, first):
        rows = pl.ds(pl.multiple_of(src * KD, 64), KD)
        for half in range(2):
            rr = pl.ds(half * GROUP, GROUP)
            xs = xb[src, rr, :]
            for n in range(0, CH, 128 * 5):
                v = dot(xs, wi[rows, :])
                acc_i[rr, :] = v if first else acc_i[rr, :] + v
            v = dot(xs, ws[rows, :])
            acc_s[rr, :] = v if first else acc_s[rr, :] + v
            v = dot(xs, wt[rows, :])
            acc_t[rr, 0:HD] = v if first else acc_t[rr, 0:HD] + v

    accumulate(tp, True)
    arrived(left, 0)
    send(left, 0, right, g_send.at[6])
    send(left, 0, partner, g_send.at[7])
    arrived(right, 1)
    send(right, 1, left, g_send.at[8])
    send(right, 1, partner, g_send.at[9])
    arrived(partner, 0)
    arrived(partner, 1)
    accumulate(partner, False)
    arrived(left, 1)
    send(left, 1, partner, g_send.at[10])
    arrived(right, 0)
    send(right, 0, partner, g_send.at[11])

    def loop_accumulate(chips, which):
        def body(i, carry):
            accumulate(2 * jnp.where(i == 0, chips[0], chips[-1]) + which, False)
            return carry

        lax.fori_loop(0, len(chips), body, 0)

    loop_accumulate((lx, rx), c)
    for half in range(2):
        arrived(2 * lx + 1 - c, half)
        arrived(2 * rx + 1 - c, half)
    loop_accumulate((lx, rx), 1 - c)
    arrived(opp, 0)
    send(opp, 0, partner, g_send.at[12])
    arrived(opp, 1)
    send(opp, 1, partner, g_send.at[13])
    accumulate(opp, False)
    arrived(2 * ox + 1 - c, 0)
    arrived(2 * ox + 1 - c, 1)
    accumulate(2 * ox + 1 - c, False)

    edge_s[:, 0:CH] = acc_i[ROWS - 16 : ROWS, :].astype(BF16)
    edge_s[:, CH:CONV] = acc_s[ROWS - 16 : ROWS, :].astype(BF16)
    edge = remote(edge_s, edge_r, e_sem.at[0], e_sem.at[1], seq=nxt)
    edge.start()
    mx[8 : 8 + ROWS, 0:CH] = acc_i[...].astype(BF16).astype(F32)
    mx[8 : 8 + ROWS, CH:CONV] = acc_s[...].astype(BF16).astype(F32)

    tri = (
        lax.broadcasted_iota(jnp.int32, (GROUP, GROUP), 0) >= lax.broadcasted_iota(jnp.int32, (GROUP, GROUP), 1)
    ).astype(F32)
    for b in range(2):
        rr = slice(b * GROUP, (b + 1) * GROUP)
        raw = acc_t[rr, :] + small[0:1, :]
        dt = jnp.maximum(raw, 0.0) + jnp.log1p(jnp.exp(-jnp.abs(raw)))
        ld = -dt * small[8:9, :]
        cum = lax.dot_general(
            tri, ld, (((1,), (0,)), ((), ())), precision=lax.Precision.HIGHEST, preferred_element_type=F32
        )
        cum_s[rr, :] = cum
        dt_s[rr, :] = dt
        cumt_s[b] = (cum * LOG2E).T[0:16, :]
        dtt_s[b] = dt.T[0:16, :]
        gexp[rr, :] = expanded(jnp.exp(cum))

    def conv(b):
        def body(j, carry):
            cols = pl.ds(pl.multiple_of(j * 128, 128), 128)

            def taps(ref, kcols):
                total = mx[pl.ds(b * GROUP + 5, GROUP), cols] * ref[0:1, kcols]
                for k in range(1, 4):
                    total = total + mx[pl.ds(b * GROUP + 5 + k, GROUP), cols] * ref[k : k + 1, kcols]
                return silu(total).astype(BF16)

            act[pl.ds(b * GROUP, GROUP), cols] = taps(kern, cols)
            return carry

        lax.fori_loop(0, CONV // 128, body, 0)

    kern = pref
    kern[0:4, 0:CH] = k_inner[...]
    kern[0:4, CH:CONV] = k_state[...]

    def contribution(b):
        rr = slice(b * GROUP, (b + 1) * GROUP)
        ending = cum_s[(b + 1) * GROUP - 1 : (b + 1) * GROUP, :]
        tail = jnp.exp(ending - cum_s[rr, :]) * dt_s[rr, :]
        scaled = (act[rr, 0:CH].astype(F32) * expanded(tail)).astype(BF16)
        inject_t = act[rr, CH : CH + ST].astype(F32).T.astype(BF16)
        return dot(inject_t, scaled)

    conv(1)
    c1 = contribution(1)
    st_f[...] = c1
    edge.wait_recv()
    halo = edge_r[8:16, :].astype(F32)
    mx[0:8, :] = jnp.where(seq == 0, 0.0, halo)
    conv(0)
    c0_s[...] = contribution(0)
    ends = jnp.concatenate([cum_s[GROUP - 1 : GROUP, :], cum_s[ROWS - 1 : ROWS, :]], axis=0)
    ends8 = jnp.concatenate([ends, jnp.zeros((6, ST), F32)], axis=0)
    end_exp = expanded(jnp.exp(ends8))
    st_bf[...] = (end_exp[1:2, :] * c0_s[...] + st_f[...]).astype(BF16)
    total = ends[0:1, :] + ends[1:2, :]
    row8 = lax.broadcasted_iota(jnp.int32, (8, ST), 0)
    t_send[...] = jnp.where(row8 == z, total, 0.0)

    def zcopy(k):
        to = (z + k) % 8
        return (
            remote(st_bf.at[pl.ds(pl.multiple_of(16 * to, 16), 16), :], z_recv.at[z], zs_sem.at[k], zr_sem.at[z],
                   seq=y * 8 + to),
            remote(t_send, t_recv.at[z], ts_sem.at[k], tr_sem.at[z], seq=y * 8 + to),
        )

    for k in range(1, 8):
        for copy in zcopy(k):
            copy.start()
            sent.append(copy)
    z_recv[z] = st_bf[pl.ds(pl.multiple_of(16 * z, 16), 16), :]
    t_recv[z] = t_send[...]

    def intra(b, rr0):
        t0 = pl.ds(rr0, 128)
        t1 = pl.ds(rr0 + 128, 128)
        both = pl.ds(rr0, GROUP)
        inject = act[both, CH : CH + ST]
        sc0 = dot_nt(act[t0, CH + ST : CONV], inject[0:128, :])
        sc1 = dot_nt(act[t1, CH + ST : CONV], inject)
        diag = lax.broadcasted_iota(jnp.int32, (128, 128), 0) >= lax.broadcasted_iota(jnp.int32, (128, 128), 1)
        lane = lax.broadcasted_iota(jnp.int32, (128, 128), 1) < 64
        ca = cum_s[t0, :] * LOG2E
        cb = cum_s[t1, :] * LOG2E
        for p in range(HD // 2):
            cols = slice(p * 128, (p + 1) * 128)
            chan = act[both, cols]
            res0, res1 = [], []
            for h in (2 * p, 2 * p + 1):
                ct = cumt_s[b, h : h + 1, :]
                dtr = dtt_s[b, h : h + 1, :]
                g0 = jnp.where(diag, ca[:, h : h + 1] - ct[:, 0:128], -1e30)
                m0 = (sc0 * jnp.exp2(g0) * dtr[:, 0:128]).astype(BF16)
                res0.append(dot(m0, chan[0:128, :]))
                g1 = cb[:, h : h + 1] - ct[:, 0:128]
                m1 = (sc1[:, 0:128] * jnp.exp2(g1) * dtr[:, 0:128]).astype(BF16)
                g2 = jnp.where(diag, cb[:, h : h + 1] - ct[:, 128:256], -1e30)
                m2 = (sc1[:, 128:256] * jnp.exp2(g2) * dtr[:, 128:256]).astype(BF16)
                res1.append(dot(m1, chan[0:128, :]) + dot(m2, chan[128:256, :]))
            ssd[t0, cols] = jnp.where(lane, res0[0], res0[1])
            ssd[t1, cols] = jnp.where(lane, res1[0], res1[1])

    def intra_body(b, carry):
        intra(b, pl.multiple_of(b * GROUP, GROUP))
        return carry

    lax.fori_loop(0, 2, intra_body, 0)

    for k in range(1, 8):
        src = (z + k) % 8
        remote(st_bf.at[0:16, :], z_recv.at[src], zs_sem.at[k], zr_sem.at[src], seq=prv).wait_recv()
        remote(t_send, t_recv.at[src], ts_sem.at[k], tr_sem.at[src], seq=prv).wait_recv()
    tall = t_recv[0]
    for k in range(1, 8):
        tall = tall + t_recv[k]
    texp = expanded(jnp.exp(tall))
    prefix = jnp.zeros((16, CH), F32)
    tsum = jnp.zeros((1, ST), F32)
    tpre = []
    for k in range(8):
        f_pre = prefix
        pref[16 * k : 16 * (k + 1), 0:CH] = f_pre
        tpre.append(tsum)
        prefix = texp[k : k + 1, :] * prefix + z_recv[k].astype(F32)
        tsum = tsum + tall[k : k + 1, :]
    y_send[...] = prefix.astype(BF16)
    yt_send[...] = jnp.where(row8 == y, tsum, 0.0)
    for k in range(1, 4):
        to = ((y + k) % 4) * 8 + z
        a = remote(y_send, y_recv.at[y], ys_sem.at[k], yr_sem.at[y], seq=to)
        b = remote(yt_send, yt_recv.at[y], yts_sem.at[k], ytr_sem.at[y], seq=to)
        for copy in (a, b):
            copy.start()
            sent.append(copy)
    y_recv[y] = y_send[...]
    yt_recv[y] = yt_send[...]

    loads[4].wait()

    def gate_body(half, carry):
        rr = pl.ds(pl.multiple_of(half * GROUP, GROUP), GROUP)
        v = dot(xb[0, rr, :], wg[0:KD, :])
        for src in range(1, 8):
            v = v + dot(xb[src, rr, :], wg[src * KD : (src + 1) * KD, :])
        acc_g[rr, :] = silu(v.astype(BF16).astype(F32))
        return carry

    lax.fori_loop(0, 2, gate_body, 0)

    for k in range(1, 4):
        src = (y + k) % 4
        remote(y_send, y_recv.at[src], ys_sem.at[k], yr_sem.at[src], seq=prv).wait_recv()
        remote(yt_send, yt_recv.at[src], yts_sem.at[k], ytr_sem.at[src], seq=prv).wait_recv()
    yall = yt_recv[0]
    for k in range(1, 4):
        yall = yall + yt_recv[k]
    yexp = expanded(jnp.exp(yall))
    run = jnp.zeros((16, CH), F32)
    chosen = run
    for k in range(3):
        run = yexp[k : k + 1, :] * run + y_recv[k].astype(F32)
        chosen = jnp.where(y == k + 1, run, chosen)
    pexp = expanded(jnp.exp(jnp.concatenate(tpre, axis=0)))
    for k in range(8):
        f_send[k] = (pref[16 * k : 16 * (k + 1), 0:CH] + pexp[k : k + 1, :] * chosen).astype(BF16)
    mine = pl.ds(pl.multiple_of(16 * z, 16), 16)
    for k in range(1, 8):
        to = (z + k) % 8
        copy = remote(f_send.at[to], inc.at[mine, :], fs_sem.at[k], fr_sem.at[z], seq=y * 8 + to)
        copy.start()
        sent.append(copy)
    inc[mine, :] = f_send[z]

    skips = expanded(small[16:24, :])[0:1, :]
    ssd[...] = ssd[...] + skips * act[:, 0:CH].astype(F32)
    loads[5].wait()

    for k in range(1, 8):
        src = (z + k) % 8
        there = pl.ds(pl.multiple_of(16 * src, 16), 16)
        remote(f_send.at[0], inc.at[there, :], fs_sem.at[k], fr_sem.at[src], seq=prv).wait_recv()
    carr[0] = inc[...]
    carr[1] = (c0_s[...] + end_exp[0:1, :] * inc[...].astype(F32)).astype(BF16)

    ones = jnp.ones((8, CH), BF16)

    def gated_body(i, carry):
        rr = pl.ds(pl.multiple_of(i * 128, 128), 128)
        reads = dot(act[rr, CH + ST : CONV], carr[i // 2])
        g = (ssd[rr, :] + reads * gexp[rr, :]) * acc_g[rr, :]
        hi, lo = split2(g * g)
        sq_send[i] = dot_nt(ones, hi) + dot_nt(ones, lo)
        gb = (g * gain[...]).astype(BF16)
        to = pl.ds(pl.multiple_of(i * 64, 64), 64)
        gated[0, to, :] = gb[0:64, :]
        gated[1, to, :] = gb[64:128, :]
        return carry

    lax.fori_loop(0, 4, gated_body, 0)
    for k in range(1, 8):
        to = (tp + k) % 8
        copy = remote(sq_send.at[to // 2], sq_recv.at[tp], qs_sem.at[k], qr_sem.at[tp], tp=to)
        copy.start()
        sent.append(copy)
    sq_recv[tp] = sq_send[x]

    def dcopy(q):
        return remote(d_send.at[q], d_recv.at[q], ds_sem.at[q], dr_sem.at[q], tp=partner)

    def block(chip):
        return pl.ds(pl.multiple_of(64 * chip, 64), 64)

    def started(copy):
        copy.start()
        sent.append(copy)

    for q in range(NQ):
        wcols = wo[:, q * QC : (q + 1) * QC]
        d_send[q] = dot(gated[1 - c], wcols).astype(BF16)
        started(dcopy(q))
        keep[q] = dot(gated[c], wcols)

    def hop1(q):
        to = right if q % 2 == 0 else left
        return remote(r1_send.at[q, 0], r1_recv.at[q], rs_sem.at[q, 0], rr_sem.at[q, 0], tp=to)

    def direct(q):
        if q % 2 == 0:
            return remote(r1_send.at[q, 1], fin_r.at[q], rs_sem.at[q, 1], rr_sem.at[q, 1], tp=left)
        return remote(r1_send.at[q, 1], fin_l.at[q], rs_sem.at[q, 1], rr_sem.at[q, 1], tp=right)

    def hop2(q):
        if q % 2 == 0:
            return remote(r2_send.at[q], fin_l.at[q], rs_sem.at[q, 2], rr_sem.at[q, 2], tp=right)
        return remote(r2_send.at[q], fin_r.at[q], rs_sem.at[q, 2], rr_sem.at[q, 2], tp=left)

    for q in range(NQ):
        dcopy(q).wait_recv()
        keep[q] = keep[q] + d_recv[q].astype(F32)
        r1_send[q, 0] = keep[q, block(ox), :].astype(BF16)
        started(hop1(q))
        other = lx if q % 2 == 0 else rx
        r1_send[q, 1] = keep[q, block(other), :].astype(BF16)
        started(direct(q))
    for q in range(NQ):
        hop1(q).wait_recv()
        ahead = rx if q % 2 == 0 else lx
        r2_send[q] = (keep[q, block(ahead), :] + r1_recv[q].astype(F32)).astype(BF16)
        started(hop2(q))

    for k in range(1, 8):
        src = (tp + k) % 8
        remote(sq_send.at[0], sq_recv.at[src], qs_sem.at[k], qr_sem.at[src], tp=partner).wait_recv()
    sq = sq_recv[0]
    for k in range(1, 8):
        sq = sq + sq_recv[k]
    factor = lax.rsqrt(sq * (1.0 / INNER) + 1e-5)
    scale_s[...] = jnp.broadcast_to(factor[0:1, :], (128, 128)).T
    scale = scale_s[block(c), :]
    for q in range(NQ):
        direct(q).wait_recv()
        hop2(q).wait_recv()
        v = keep[q, block(x), :] + fin_l[q].astype(F32) + fin_r[q].astype(F32)
        for j in range(QC // 128):
            cols = slice(j * 128, (j + 1) * 128)
            out[:, q * QC + j * 128 : q * QC + (j + 1) * 128] = (v[:, cols] * scale).astype(BF16)
    edge.wait_send()
    for copy in sent:
        copy.wait_send()


def on_device(tok, w_gate, w_inner, w_state, w_step, k_inner, k_state, bias, rate, skip, gain, w_out):
    vm = pltpu.VMEM
    dma = pltpu.SemaphoreType.DMA
    scratch = [
        vm((8, ROWS, KD), BF16), vm((D, CH), BF16), vm((D, CH), BF16), vm((D, 2 * ST), BF16), vm((D, HD), BF16),
        vm((CH, D), BF16),
        vm((ROWS, CH), F32), vm((ROWS, 2 * ST), F32), vm((ROWS, ST), F32), vm((ROWS, CH), F32),
        vm((8 + ROWS, CONV), F32), vm((ROWS, CONV), BF16), vm((16, CONV), BF16), vm((16, CONV), BF16),
        vm((24, ST), F32), vm((ST, CH), BF16), vm((ROWS, ST), F32), vm((ROWS, ST), F32),
        vm((2, 16, GROUP), F32), vm((2, 16, GROUP), F32),
        vm((ROWS, CH), F32), vm((ROWS, CH), F32), vm((ST, CH), BF16), vm((ST, CH), F32), vm((ST, CH), F32),
        vm((8, 16, CH), BF16), vm((8, ST), F32), vm((8, 8, ST), F32), vm((ST, CONV), F32),
        vm((16, CH), BF16), vm((8, ST), F32), vm((4, 16, CH), BF16), vm((4, 8, ST), F32),
        vm((8, 16, CH), BF16), vm((ST, CH), BF16), vm((2, ST, CH), BF16),
        vm((2, GROUP, CH), BF16), vm((4, 8, ST), F32), vm((8, 8, ST), F32),
        vm((NQ, GROUP, QC), F32), vm((NQ, GROUP, QC), BF16), vm((NQ, GROUP, QC), BF16),
        vm((NQ, 2, 64, QC), BF16), vm((NQ, 64, QC), BF16), vm((NQ, 64, QC), BF16),
        vm((NQ, 64, QC), BF16), vm((NQ, 64, QC), BF16), vm((128, 128), F32),
        dma((6,)), dma((14,)), dma((8, 2)), dma((2,)), dma((8,)), dma((8,)), dma((8,)), dma((8,)),
        dma((4,)), dma((4,)), dma((4,)), dma((4,)), dma((8,)), dma((8,)),
        dma((8,)), dma((8,)), dma((NQ,)), dma((NQ,)), dma((NQ, 3)), dma((NQ, 3)),
    ]
    hbm = pl.BlockSpec(memory_space=pl.ANY)
    local = pl.BlockSpec(memory_space=pltpu.VMEM)
    return pl.pallas_call(
        kernel,
        name="layer",
        out_shape=jax.ShapeDtypeStruct((ROWS // 8, D), BF16),
        in_specs=[hbm] * 5 + [local] * 6 + [hbm],
        out_specs=local,
        scratch_shapes=scratch,
        compiler_params=pltpu.CompilerParams(
            collective_id=0, has_side_effects=True, vmem_limit_bytes=62 * 1024 * 1024
        ),
    )(
        tok, w_gate, w_inner, w_state, w_step, k_inner, k_state,
        bias.reshape(1, -1), rate.reshape(1, -1), skip.reshape(1, -1), gain.reshape(1, -1), w_out,
    )


def solution(mesh):
    return jax.shard_map(
        on_device,
        mesh=mesh,
        in_specs=(
            P("seq", "tp"), P(None, "tp"), P(None, "tp"), P(), P(None, "tp"), P(None, "tp"), P(),
            P("tp"), P("tp"), P("tp"), P("tp"), P("tp", None),
        ),
        out_specs=P(("seq", "tp"), None),
        check_vma=False,
    )
```

time: 208 us -> 77.9 us (0.37)
  the two profiles are of different devices: /device:TPU:1 before, /device:TPU:4 now
where the time goes in v1:
time: 77.9 us; the launch traced here: 77.7 us
  Pallas kernels  70.8 us (91%)
  local copies, waits for them, and re-layouts  6.9 us (9%)
    pallas_call x1, Pallas kernels, on_device(): pl.pallas_call(kernel, name='layer', out_shape=jax.ShapeDtypeStruct((ROWS...  70.8 us
    unnamed x3, local copies, waits for them, and re-layouts  5.63 us

profile of v1, /device:TPU:4, one launch (start us, length us, event | category | flops | bytes accessed | tf_op | source)
XLA Modules:
  0.0 77.7 jit_solution(754535404692392550)
XLA Ops:
  0.0 1.3 %reshape.15.gain = f32[1,640]{1,0:T(1,128)} reshape(f32[640]{0:T(1024)} %param.22) | data formatting | bytes 5120 | tf_op jit(solution)/shard_map/reshape | solution.py:495
  1.3 1.9 %copy.13.tok = bf16[512,320]{1,0:T(8,128)(2,1)} copy(bf16[512,320]{0,1:T(8,128)(2,1)} %param.12) | data formatting | bytes 655360 | tf_op args[0]
  3.2 2.0 %copy.14.w_step = bf16[2560,10]{1,0:T(8,128)(2,1)} copy(bf16[2560,10]{0,1:T(8,128)(2,1)} %param.16) | data formatting | bytes 102400 | tf_op args[4]
  5.2 70.8 %layer.1 = bf16[64,2560]{1,0:T(8,128)(2,1)} custom-call(bf16[512,320]{1,0:T(8,128)(2,1)} %copy.13.tok, bf16[2560,640]{1,0:T(8,128)(2,1)} %w_gate.1, bf16[2560,640]{1,0:T(8,128)(2,1)} %w_inner.1, bf16[2560,256]{1,0:T(8,128)(2,1)} %w_state.1, bf16[2560,10]{1,0:T(8,128)(2,1)} %copy.14.w_step, f32[4,640]{1,0:T(4,128)} %k_inner.1, f32[4,256]{1,0:T(4,128)} %k_state.1, ...), custom_call_target="tpu_custom_call" | custom-call | tf_op jit(solution)/shard_map/layer/pallas_call | solution.py:483
  75.9 1.7 %copy.16 = bf16[64,2560]{1,0:T(8,128)(2,1)} copy(bf16[64,2560]{1,0:T(8,128)(2,1)} %layer.1) | data formatting | bytes 655360

commit v2 on v1

v2 whole, which is shorter than its diff:
```python
import jax
import jax.numpy as jnp
from jax import lax
from jax.experimental import pallas as pl
from jax.experimental.pallas import tpu as pltpu
from jax.sharding import PartitionSpec as P

MESH = pl.DeviceIdType.MESH
F32 = jnp.float32
BF16 = jnp.bfloat16
ROWS = 512
GROUP = 256
KD = 320
D = 2560
CH = 640
HD = 10
ST = 128
CONV = CH + 2 * ST
WIDE = CONV + ST
CUTS = ((0, 512), (1280, 512), (512, 768), (1792, 768))
NQ = len(CUTS)
QC = 768
LOG2E = 1.4426950408889634
INNER = 5120


def split2(v):
    hi = v.astype(BF16)
    return hi, (v - hi.astype(F32)).astype(BF16)


def dot(a, b):
    return jnp.dot(a, b, preferred_element_type=F32)


def dot_nt(a, b):
    return lax.dot_general(a, b, (((1,), (1,)), ((), ())), preferred_element_type=F32)


class Phases:
    open_scope = None

    def __call__(self, name):
        self.close()
        self.open_scope = jax.named_scope(name)
        self.open_scope.__enter__()

    def close(self):
        if self.open_scope is not None:
            self.open_scope.__exit__(None, None, None)
            self.open_scope = None


def silu(v):
    return 0.5 * v * (1.0 + jnp.tanh(0.5 * v))


def kernel(
    tok, w_gate, w_inner, w_state, w_step, k_inner, k_state, bias, rate, skip, gain, w_out,
    out,
    xb, tok_t, step_t, step_f, wg, wall, wo, kern, vec, gain_v,
    acc, acc_g, mx, act, edge_s, edge_r,
    small, expand, cum_s, dt_s, cumt_s, dtt_s,
    ssd, gexp, st_bf, st_f, c0_s, z_recv, t_send, t_recv, pref, y_send, yt_send, y_recv, yt_recv, f_send, inc, carr,
    sq_send, sq_recv, both, keep, d_send, d_recv, r1_send, r1_recv, fin_l, fin_r, scale_s,
    loc_sem, g_send, g_recv, e_sem, zs_sem, zr_sem, ts_sem, tr_sem, ys_sem, yr_sem, yts_sem, ytr_sem, fs_sem, fr_sem,
    qs_sem, qr_sem, ds_sem, dr_sem, rs_sem, rr_sem,
):
    seq = lax.axis_index("seq")
    tp = lax.axis_index("tp")
    x = tp // 2
    c = tp % 2
    y = seq // 8
    z = seq % 8
    partner = 2 * x + (1 - c)
    rx, lx, ox = (x + 1) % 4, (x + 3) % 4, (x + 2) % 4
    right, left, opp = 2 * rx + c, 2 * lx + c, 2 * ox + c
    nxt, prv = (seq + 1) % 32, (seq + 31) % 32

    def remote(src, dst, ssem, rsem, **where):
        return pltpu.make_async_remote_copy(
            src_ref=src, dst_ref=dst, send_sem=ssem, recv_sem=rsem, device_id=where, device_id_type=MESH
        )

    phase = Phases()
    phase("start")
    copies = (
        (tok, tok_t), (w_inner, wall.at[:, 0:CH]), (w_state, wall.at[:, CH:CONV]), (w_step, step_t),
        (k_inner, kern.at[:, 0:CH]), (k_state, kern.at[:, CH:CONV]), (bias, vec.at[0:1]), (rate, vec.at[1:2]),
        (skip, vec.at[2:3]), (gain, gain_v), (w_gate, wg), (w_out, wo),
    )
    loads = [pltpu.make_async_copy(src, dst, loc_sem.at[i]) for i, (src, dst) in enumerate(copies)]
    for load in loads:
        load.start()

    barrier = pltpu.get_barrier_semaphore()
    for k in range(1, 8):
        pl.semaphore_signal(barrier, inc=1, device_id={"tp": (tp + k) % 8}, device_id_type=MESH)
    for k in range(1, 8):
        pl.semaphore_signal(barrier, inc=1, device_id={"seq": y * 8 + (z + k) % 8}, device_id_type=MESH)
    for k in range(1, 4):
        pl.semaphore_signal(barrier, inc=1, device_id={"seq": ((y + k) % 4) * 8 + z}, device_id_type=MESH)
    for s in (nxt, prv):
        pl.semaphore_signal(barrier, inc=1, device_id={"seq": s}, device_id_type=MESH)

    er = lax.broadcasted_iota(jnp.int32, (ST, CH), 0)
    ec = lax.broadcasted_iota(jnp.int32, (ST, CH), 1)
    off = ec - er * 64
    expand[...] = jnp.where((off >= 0) & (off < 64), 1.0, 0.0).astype(BF16)
    small[...] = jnp.zeros_like(small)

    def expanded(v):
        hi, lo = split2(v)
        return dot(hi, expand[...]) + dot(lo, expand[...])

    phase("turn")
    loads[0].wait()
    xb[tp] = tok_t[...].T
    phase("barrier")
    pl.semaphore_wait(barrier, 19)

    phase("send")
    def piece(src, half, to, ssem):
        part = xb.at[src, pl.ds(half * GROUP, GROUP), :]
        return remote(part, part, ssem, g_recv.at[src, half], tp=to)

    sent = []

    def send(src, half, to, ssem):
        copy = piece(src, half, to, ssem)
        copy.start()
        sent.append(copy)

    def arrived(src, half):
        piece(src, half, partner, g_send.at[0]).wait_recv()

    send(tp, 0, right, g_send.at[0])
    send(tp, 1, left, g_send.at[1])
    send(tp, 1, right, g_send.at[2])
    send(tp, 0, left, g_send.at[3])
    send(tp, 0, partner, g_send.at[4])
    send(tp, 1, partner, g_send.at[5])
    phase("step_turn")
    loads[3].wait()
    step_f[...] = jnp.zeros_like(step_f)
    step_f[0:HD, :] = step_t[...].astype(F32)
    wall[:, CONV:WIDE] = step_f[...].T.astype(BF16)
    for i in (6, 7, 8):
        loads[i].wait()
        small[8 * (i - 6) : 8 * (i - 6) + 1, 0:HD] = vec[i - 6 : i - 5, :]
    loads[1].wait()
    loads[2].wait()

    def accumulate(src, half, first=False):
        rr = pl.ds(half * GROUP, GROUP)
        v = dot(xb[src, rr, :], wall[pl.ds(pl.multiple_of(src * KD, 64), KD), :])
        acc[rr, :] = v if first else acc[rr, :] + v

    rp, lp, op = 2 * rx + 1 - c, 2 * lx + 1 - c, 2 * ox + 1 - c
    phase("own")
    accumulate(tp, 0, True)
    accumulate(tp, 1, True)
    for half in range(2):
        arrived(partner, half)
        accumulate(partner, half)
    phase("near0")
    arrived(left, 0)
    send(left, 0, right, g_send.at[6])
    send(left, 0, partner, g_send.at[7])
    arrived(right, 1)
    send(right, 1, left, g_send.at[8])
    send(right, 1, partner, g_send.at[9])
    phase("near0_acc")
    accumulate(left, 0)
    accumulate(right, 1)
    arrived(lp, 0)
    accumulate(lp, 0)
    arrived(rp, 1)
    accumulate(rp, 1)
    phase("near1")
    arrived(left, 1)
    send(left, 1, partner, g_send.at[10])
    arrived(right, 0)
    send(right, 0, partner, g_send.at[11])
    phase("near1_acc")
    accumulate(left, 1)
    accumulate(right, 0)
    arrived(lp, 1)
    accumulate(lp, 1)
    arrived(rp, 0)
    accumulate(rp, 0)
    phase("far")
    arrived(opp, 0)
    send(opp, 0, partner, g_send.at[12])
    arrived(opp, 1)
    send(opp, 1, partner, g_send.at[13])
    phase("far_acc")
    accumulate(opp, 0)
    accumulate(opp, 1)
    phase("far_p")
    for half in range(2):
        arrived(op, half)
        accumulate(op, half)

    phase("edge")
    edge_s[...] = acc[ROWS - 16 : ROWS, 0:CONV].astype(BF16)
    edge = remote(edge_s, edge_r, e_sem.at[0], e_sem.at[1], seq=nxt)
    edge.start()
    mx[8 : 8 + ROWS, :] = acc[:, 0:CONV].astype(BF16).astype(F32)

    phase("steps")
    tri = (
        lax.broadcasted_iota(jnp.int32, (GROUP, GROUP), 0) >= lax.broadcasted_iota(jnp.int32, (GROUP, GROUP), 1)
    ).astype(F32)
    for b in range(2):
        rr = slice(b * GROUP, (b + 1) * GROUP)
        raw = acc[rr, CONV:WIDE] + small[0:1, :]
        dt = jnp.maximum(raw, 0.0) + jnp.log1p(jnp.exp(-jnp.abs(raw)))
        ld = -dt * small[8:9, :]
        cum = lax.dot_general(
            tri, ld, (((1,), (0,)), ((), ())), precision=lax.Precision.HIGHEST, preferred_element_type=F32
        )
        cum_s[rr, :] = cum
        dt_s[rr, :] = dt
    ends = jnp.concatenate([cum_s[GROUP - 1 : GROUP, :], cum_s[ROWS - 1 : ROWS, :]], axis=0)
    total = ends[0:1, :] + ends[1:2, :]
    row8 = lax.broadcasted_iota(jnp.int32, (8, ST), 0)
    t_send[...] = jnp.where(row8 == z, total, 0.0)

    def tcopy(k):
        return remote(t_send, t_recv.at[z], ts_sem.at[k], tr_sem.at[z], seq=y * 8 + (z + k) % 8)

    for k in range(1, 8):
        tcopy(k).start()
        sent.append(tcopy(k))
    t_recv[z] = t_send[...]

    def conv(b):
        def body(j, carry):
            cols = pl.ds(pl.multiple_of(j * 128, 128), 128)

            def taps(ref, kcols):
                total = mx[pl.ds(b * GROUP + 5, GROUP), cols] * ref[0:1, kcols]
                for k in range(1, 4):
                    total = total + mx[pl.ds(b * GROUP + 5 + k, GROUP), cols] * ref[k : k + 1, kcols]
                return silu(total).astype(BF16)

            act[pl.ds(b * GROUP, GROUP), cols] = taps(kern, cols)
            return carry

        lax.fori_loop(0, CONV // 128, body, 0)

    loads[4].wait()
    loads[5].wait()

    def contribution(b):
        rr = slice(b * GROUP, (b + 1) * GROUP)
        ending = cum_s[(b + 1) * GROUP - 1 : (b + 1) * GROUP, :]
        tail = jnp.exp(ending - cum_s[rr, :]) * dt_s[rr, :]
        scaled = (act[rr, 0:CH].astype(F32) * expanded(tail)).astype(BF16)
        inject_t = act[rr, CH : CH + ST].astype(F32).T.astype(BF16)
        return dot(inject_t, scaled)

    phase("conv1")
    conv(1)
    phase("contrib1")
    c1 = contribution(1)
    st_f[...] = c1
    phase("edge_wait")
    edge.wait_recv()
    halo = edge_r[8:16, :].astype(F32)
    mx[0:8, :] = jnp.where(seq == 0, 0.0, halo)
    phase("conv0")
    conv(0)
    phase("contrib0")
    c0_s[...] = contribution(0)
    ends8 = jnp.concatenate([ends, jnp.zeros((6, ST), F32)], axis=0)
    end_exp = expanded(jnp.exp(ends8))
    st_bf[...] = (end_exp[1:2, :] * c0_s[...] + st_f[...]).astype(BF16)
    phase("zsend")
    def zcopy(k):
        to = (z + k) % 8
        return remote(st_bf.at[pl.ds(pl.multiple_of(16 * to, 16), 16), :], z_recv.at[z], zs_sem.at[k], zr_sem.at[z],
                      seq=y * 8 + to)

    for k in (4, 3, 5, 2, 6, 1, 7):
        zcopy(k).start()
        sent.append(zcopy(k))
    z_recv[z] = st_bf[pl.ds(pl.multiple_of(16 * z, 16), 16), :]

    phase("late_steps")
    for b in range(2):
        rr = slice(b * GROUP, (b + 1) * GROUP)
        cumt_s[b] = (cum_s[rr, :] * LOG2E).T[0:16, :]
        dtt_s[b] = dt_s[rr, :].T[0:16, :]
        gexp[rr, :] = expanded(jnp.exp(cum_s[rr, :]))

    def intra(b, rr0):
        t0 = pl.ds(rr0, 128)
        t1 = pl.ds(rr0 + 128, 128)
        both = pl.ds(rr0, GROUP)
        inject = act[both, CH : CH + ST]
        sc0 = dot_nt(act[t0, CH + ST : CONV], inject[0:128, :])
        sc1 = dot_nt(act[t1, CH + ST : CONV], inject)
        diag = lax.broadcasted_iota(jnp.int32, (128, 128), 0) >= lax.broadcasted_iota(jnp.int32, (128, 128), 1)
        lane = lax.broadcasted_iota(jnp.int32, (128, 128), 1) < 64
        ca = cum_s[t0, :] * LOG2E
        cb = cum_s[t1, :] * LOG2E
        for p in range(HD // 2):
            cols = slice(p * 128, (p + 1) * 128)
            chan = act[both, cols]
            res0, res1 = [], []
            for h in (2 * p, 2 * p + 1):
                ct = cumt_s[b, h : h + 1, :]
                dtr = dtt_s[b, h : h + 1, :]
                g0 = jnp.where(diag, ca[:, h : h + 1] - ct[:, 0:128], -1e30)
                m0 = (sc0 * jnp.exp2(g0) * dtr[:, 0:128]).astype(BF16)
                res0.append(dot(m0, chan[0:128, :]))
                g1 = cb[:, h : h + 1] - ct[:, 0:128]
                m1 = (sc1[:, 0:128] * jnp.exp2(g1) * dtr[:, 0:128]).astype(BF16)
                g2 = jnp.where(diag, cb[:, h : h + 1] - ct[:, 128:256], -1e30)
                m2 = (sc1[:, 128:256] * jnp.exp2(g2) * dtr[:, 128:256]).astype(BF16)
                res1.append(dot(m1, chan[0:128, :]) + dot(m2, chan[128:256, :]))
            ssd[t0, cols] = jnp.where(lane, res0[0], res0[1])
            ssd[t1, cols] = jnp.where(lane, res1[0], res1[1])

    def intra_body(b, carry):
        intra(b, pl.multiple_of(b * GROUP, GROUP))
        return carry

    phase("intra")
    lax.fori_loop(0, 2, intra_body, 0)

    phase("zwait")
    for k in range(1, 8):
        src = (z + k) % 8
        remote(st_bf.at[0:16, :], z_recv.at[src], zs_sem.at[k], zr_sem.at[src], seq=prv).wait_recv()
        remote(t_send, t_recv.at[src], ts_sem.at[k], tr_sem.at[src], seq=prv).wait_recv()
    phase("prefix")
    tall = t_recv[0]
    for k in range(1, 8):
        tall = tall + t_recv[k]
    texp = expanded(jnp.exp(tall))
    prefix = jnp.zeros((16, CH), F32)
    tsum = jnp.zeros((1, ST), F32)
    tpre = []
    for k in range(8):
        f_pre = prefix
        pref[16 * k : 16 * (k + 1), 0:CH] = f_pre
        tpre.append(tsum)
        prefix = texp[k : k + 1, :] * prefix + z_recv[k].astype(F32)
        tsum = tsum + tall[k : k + 1, :]
    y_send[...] = prefix.astype(BF16)
    yt_send[...] = jnp.where(row8 == y, tsum, 0.0)
    for k in range(1, 4):
        to = ((y + k) % 4) * 8 + z
        a = remote(y_send, y_recv.at[y], ys_sem.at[k], yr_sem.at[y], seq=to)
        b = remote(yt_send, yt_recv.at[y], yts_sem.at[k], ytr_sem.at[y], seq=to)
        for copy in (a, b):
            copy.start()
            sent.append(copy)
    y_recv[y] = y_send[...]
    yt_recv[y] = yt_send[...]

    phase("gate")
    loads[10].wait()

    def gate_body(half, carry):
        rr = pl.ds(pl.multiple_of(half * GROUP, GROUP), GROUP)
        v = dot(xb[0, rr, :], wg[0:KD, :])
        for src in range(1, 8):
            v = v + dot(xb[src, rr, :], wg[src * KD : (src + 1) * KD, :])
        acc_g[rr, :] = silu(v.astype(BF16).astype(F32))
        return carry

    lax.fori_loop(0, 2, gate_body, 0)
    phase("ywait")

    for k in range(1, 4):
        src = (y + k) % 4
        remote(y_send, y_recv.at[src], ys_sem.at[k], yr_sem.at[src], seq=prv).wait_recv()
        remote(yt_send, yt_recv.at[src], yts_sem.at[k], ytr_sem.at[src], seq=prv).wait_recv()
    phase("ycomb")
    yall = yt_recv[0]
    for k in range(1, 4):
        yall = yall + yt_recv[k]
    yexp = expanded(jnp.exp(yall))
    run = jnp.zeros((16, CH), F32)
    chosen = run
    for k in range(3):
        run = yexp[k : k + 1, :] * run + y_recv[k].astype(F32)
        chosen = jnp.where(y == k + 1, run, chosen)
    pexp = expanded(jnp.exp(jnp.concatenate(tpre, axis=0)))
    for k in range(8):
        f_send[k] = (pref[16 * k : 16 * (k + 1), 0:CH] + pexp[k : k + 1, :] * chosen).astype(BF16)
    mine = pl.ds(pl.multiple_of(16 * z, 16), 16)
    for k in (4, 3, 5, 2, 6, 1, 7):
        to = (z + k) % 8
        copy = remote(f_send.at[to], inc.at[mine, :], fs_sem.at[k], fr_sem.at[z], seq=y * 8 + to)
        copy.start()
        sent.append(copy)
    inc[mine, :] = f_send[z]

    phase("skip")
    skips = expanded(small[16:24, :])[0:1, :]
    ssd[...] = ssd[...] + skips * act[:, 0:CH].astype(F32)
    loads[9].wait()
    loads[11].wait()
    phase("fwait")

    for k in range(1, 8):
        src = (z + k) % 8
        there = pl.ds(pl.multiple_of(16 * src, 16), 16)
        remote(f_send.at[0], inc.at[there, :], fs_sem.at[k], fr_sem.at[src], seq=prv).wait_recv()
    phase("gated")
    carr[0] = inc[...]
    carr[1] = (c0_s[...] + end_exp[0:1, :] * inc[...].astype(F32)).astype(BF16)

    ones = jnp.ones((8, CH), BF16)
    gain_row = gain_v[...].reshape(1, CH)

    def gate(chip):
        rr = pl.ds(pl.multiple_of(chip * 128, 128), 128)
        reads = dot(act[rr, CH + ST : CONV], carr[chip // 2])
        g = (ssd[rr, :] + reads * gexp[rr, :]) * acc_g[rr, :]
        hi, lo = split2(g * g)
        sq_send[chip] = dot_nt(ones, hi) + dot_nt(ones, lo)
        return (g * gain_row).astype(BF16)

    def started(copy):
        copy.start()
        sent.append(copy)

    def part(ref, *at):
        return ref.at[at + (slice(None), pl.ds(0, CUTS[at[-1]][1]))]

    def dcopy(j, q):
        return remote(part(d_send, j, q), part(d_recv, j, q), ds_sem.at[j, q], dr_sem.at[j, q], tp=partner)

    def project(j, rows):
        for q, (start, width) in enumerate(CUTS):
            cols = pl.ds(0, width)
            v = dot(rows, wo[:, start : start + width])
            both[0, :, cols] = v[0:64, :]
            both[1, :, cols] = v[64:128, :]
            d_send[j, q, :, cols] = both[1 - c, :, cols].astype(BF16)
            started(dcopy(j, q))
            keep[j, q, :, cols] = both[c, :, cols]

    def paired(j, q):
        dcopy(j, q).wait_recv()
        cols = pl.ds(0, CUTS[q][1])
        return keep[j, q, :, cols] + d_recv[j, q, :, cols].astype(F32)

    def hop1(q):
        to = right if q % 2 == 0 else left
        return remote(part(r1_send, 0, q), part(r1_recv, q), rs_sem.at[q, 0], rr_sem.at[q, 0], tp=to)

    def direct(q):
        if q % 2 == 0:
            return remote(part(r1_send, 1, q), part(fin_r, q), rs_sem.at[q, 1], rr_sem.at[q, 1], tp=left)
        return remote(part(r1_send, 1, q), part(fin_l, q), rs_sem.at[q, 1], rr_sem.at[q, 1], tp=right)

    def hop2(q):
        if q % 2 == 0:
            return remote(part(r1_send, 2, q), part(fin_l, q), rs_sem.at[q, 2], rr_sem.at[q, 2], tp=right)
        return remote(part(r1_send, 2, q), part(fin_r, q), rs_sem.at[q, 2], rr_sem.at[q, 2], tp=left)

    def put(which, q, value):
        r1_send[which, q, :, pl.ds(0, CUTS[q][1])] = value.astype(BF16)

    project(0, gate(ox))
    phase("block1")
    rows = gate(lx)
    phase("hop1")
    for q in range(NQ):
        put(0, q, paired(0, q))
        started(hop1(q))
    phase("block1_mm")
    project(1, rows)
    phase("block2")
    project(2, gate(rx))
    phase("direct")
    for q in range(NQ):
        put(1, q, paired(1 if q % 2 == 0 else 2, q))
        started(direct(q))
    phase("block3")
    project(3, gate(x))
    for k in range(1, 8):
        to = (tp + k) % 8
        started(remote(sq_send.at[to // 2], sq_recv.at[tp], qs_sem.at[k], qr_sem.at[tp], tp=to))
    sq_recv[tp] = sq_send[x]
    phase("hop2")
    for q in range(NQ):
        v = paired(2 if q % 2 == 0 else 1, q)
        hop1(q).wait_recv()
        put(2, q, v + r1_recv[q, :, pl.ds(0, CUTS[q][1])].astype(F32))
        started(hop2(q))
    phase("own_sum")
    for q in range(NQ):
        keep[3, q, :, pl.ds(0, CUTS[q][1])] = paired(3, q)
    phase("scale")
    for k in range(1, 8):
        src = (tp + k) % 8
        remote(sq_send.at[0], sq_recv.at[src], qs_sem.at[k], qr_sem.at[src], tp=partner).wait_recv()
    sq = sq_recv[0]
    for k in range(1, 8):
        sq = sq + sq_recv[k]
    factor = lax.rsqrt(sq * (1.0 / INNER) + 1e-5)
    scale_s[...] = jnp.broadcast_to(factor[0:1, :], (128, 128)).T
    scale = scale_s[pl.ds(pl.multiple_of(64 * c, 64), 64), :]
    for q, (start, width) in enumerate(CUTS):
        direct(q).wait_recv()
        hop2(q).wait_recv()
        for j in range(width // 128):
            cols = slice(j * 128, (j + 1) * 128)
            v = keep[3, q, :, cols] + fin_l[q, :, cols].astype(F32) + fin_r[q, :, cols].astype(F32)
            out[:, start + j * 128 : start + (j + 1) * 128] = (v * scale).astype(BF16)
    phase("drain")
    edge.wait_send()
    for copy in sent:
        copy.wait_send()
    phase.close()


def on_device(tok, w_gate, w_inner, w_state, w_step, k_inner, k_state, bias, rate, skip, gain, w_out):
    vm = pltpu.VMEM
    dma = pltpu.SemaphoreType.DMA
    scratch = [
        vm((8, ROWS, KD), BF16), vm((KD, ROWS), BF16), vm((HD, D), BF16), vm((ST, D), F32), vm((D, CH), BF16), vm((D, WIDE), BF16),
        vm((CH, D), BF16), vm((4, CONV), F32), vm((3, HD), F32), vm((CH,), F32),
        vm((ROWS, WIDE), F32), vm((ROWS, CH), F32),
        vm((8 + ROWS, CONV), F32), vm((ROWS, CONV), BF16), vm((16, CONV), BF16), vm((16, CONV), BF16),
        vm((24, ST), F32), vm((ST, CH), BF16), vm((ROWS, ST), F32), vm((ROWS, ST), F32),
        vm((2, 16, GROUP), F32), vm((2, 16, GROUP), F32),
        vm((ROWS, CH), F32), vm((ROWS, CH), F32), vm((ST, CH), BF16), vm((ST, CH), F32), vm((ST, CH), F32),
        vm((8, 16, CH), BF16), vm((8, ST), F32), vm((8, 8, ST), F32), vm((ST, CONV), F32),
        vm((16, CH), BF16), vm((8, ST), F32), vm((4, 16, CH), BF16), vm((4, 8, ST), F32),
        vm((8, 16, CH), BF16), vm((ST, CH), BF16), vm((2, ST, CH), BF16),
        vm((4, 8, ST), F32), vm((8, 8, ST), F32), vm((2, 64, QC), F32),
        vm((4, NQ, 64, QC), F32), vm((4, NQ, 64, QC), BF16), vm((4, NQ, 64, QC), BF16),
        vm((3, NQ, 64, QC), BF16), vm((NQ, 64, QC), BF16),
        vm((NQ, 64, QC), BF16), vm((NQ, 64, QC), BF16), vm((128, 128), F32),
        dma((12,)), dma((14,)), dma((8, 2)), dma((2,)), dma((8,)), dma((8,)), dma((8,)), dma((8,)),
        dma((4,)), dma((4,)), dma((4,)), dma((4,)), dma((8,)), dma((8,)),
        dma((8,)), dma((8,)), dma((4, NQ)), dma((4, NQ)), dma((NQ, 3)), dma((NQ, 3)),
    ]
    hbm = pl.BlockSpec(memory_space=pl.ANY)
    local = pl.BlockSpec(memory_space=pltpu.VMEM)
    return pl.pallas_call(
        kernel,
        name="layer",
        out_shape=jax.ShapeDtypeStruct((ROWS // 8, D), BF16),
        in_specs=[hbm] * 12,
        out_specs=local,
        scratch_shapes=scratch,
        compiler_params=pltpu.CompilerParams(
            collective_id=0, has_side_effects=True, vmem_limit_bytes=62 * 1024 * 1024
        ),
    )(
        tok.T, w_gate, w_inner, w_state, w_step.T, k_inner, k_state,
        bias.reshape(1, -1), rate.reshape(1, -1), skip.reshape(1, -1), gain, w_out,
    )


def solution(mesh):
    return jax.shard_map(
        on_device,
        mesh=mesh,
        in_specs=(
            P("seq", "tp"), P(None, "tp"), P(None, "tp"), P(), P(None, "tp"), P(None, "tp"), P(),
            P("tp"), P("tp"), P("tp"), P("tp"), P("tp", None),
        ),
        out_specs=P(("seq", "tp"), None),
        check_vma=False,
    )
```

time: 77.9 us -> 66.8 us (0.86)
  the two profiles are of different devices: /device:TPU:4 before, /device:TPU:1 now
where the time goes in v2:
time: 66.8 us; the launch traced here: 66.7 us
  Pallas kernels  64.9 us (97%)
  local copies, waits for them, and re-layouts  1.72 us (3%)
    pallas_call x1, Pallas kernels, on_device(): pl.pallas_call(kernel, name='layer', out_shape=jax.ShapeDtypeStruct((ROWS...  64.9 us
    unnamed x1, local copies, waits for them, and re-layouts  1.72 us

profile of v2, /device:TPU:1, one launch (start us, length us, event | category | flops | bytes accessed | tf_op | source)
XLA Modules:
  0.0 66.7 jit_solution(17698487642113132379)
XLA Ops:
  0.0 64.9 %layer.1 = bf16[64,2560]{1,0:T(8,128)(2,1)} custom-call(bf16[320,512]{1,0:T(8,128)(2,1)} %bitcast.5, bf16[2560,640]{1,0:T(8,128)(2,1)} %w_gate.1, bf16[2560,640]{1,0:T(8,128)(2,1)} %w_inner.1, bf16[2560,256]{1,0:T(8,128)(2,1)} %w_state.1, bf16[10,2560]{1,0:T(8,128)(2,1)} %bitcast.6, f32[4,640]{1,0:T(4,128)} %k_inner.1, f32[4,256]{1,0:T(4,128)} %k_state.1, ...), custom_call_target="tpu_custom_call" | custom-call | tf_op jit(solution)/shard_map/layer/pallas_call | solution.py:550
  64.9 1.7 %copy.14 = bf16[64,2560]{1,0:T(8,128)(2,1)} copy(bf16[64,2560]{1,0:T(8,128)(2,1)} %layer.1) | data formatting | bytes 655360

commit v3 on v2

--- a/solution.py
+++ b/solution.py
@@ -19,6 +19,8 @@
 WIDE = CONV + ST
 CUTS = ((0, 512), (1280, 512), (512, 768), (1792, 768))
 NQ = len(CUTS)
+PIECES = ((0, 112), (112, 128), (240, 144), (384, 128))
+EARLY = 240
 QC = 768
 LOG2E = 1.4426950408889634
 INNER = 5120
@@ -120,26 +122,29 @@
     pl.semaphore_wait(barrier, 19)
 
     phase("send")
-    def piece(src, half, to, ssem):
-        part = xb.at[src, pl.ds(half * GROUP, GROUP), :]
-        return remote(part, part, ssem, g_recv.at[src, half], tp=to)
-
     sent = []
 
-    def send(src, half, to, ssem):
-        copy = piece(src, half, to, ssem)
+    def piece(src, q, to, ssem):
+        start, rows = PIECES[q]
+        part = xb.at[src, pl.ds(start, rows), :]
+        return remote(part, part, ssem, g_recv.at[src, q], tp=to)
+
+    gathered = []
+
+    def send(src, q, to):
+        copy = piece(src, q, to, g_send.at[len(gathered)])
         copy.start()
+        gathered.append(copy)
         sent.append(copy)
 
-    def arrived(src, half):
-        piece(src, half, partner, g_send.at[0]).wait_recv()
-
-    send(tp, 0, right, g_send.at[0])
-    send(tp, 1, left, g_send.at[1])
-    send(tp, 1, right, g_send.at[2])
-    send(tp, 0, left, g_send.at[3])
-    send(tp, 0, partner, g_send.at[4])
-    send(tp, 1, partner, g_send.at[5])
+    def arrived(src, q):
+        piece(src, q, partner, g_send.at[0]).wait_recv()
+
+    for a, b in ((2, 3), (3, 2), (0, 1)):
+        send(tp, a, right)
+        send(tp, b, left)
+    for q in (2, 3, 0, 1):
+        send(tp, q, partner)
     phase("step_turn")
     loads[3].wait()
     step_f[...] = jnp.zeros_like(step_f)
@@ -151,68 +156,72 @@
     loads[1].wait()
     loads[2].wait()
 
-    def accumulate(src, half, first=False):
-        rr = pl.ds(half * GROUP, GROUP)
+    def accumulate(src, start, rows, first=False):
+        rr = pl.ds(start, rows)
         v = dot(xb[src, rr, :], wall[pl.ds(pl.multiple_of(src * KD, 64), KD), :])
         acc[rr, :] = v if first else acc[rr, :] + v
 
+    early, late = (EARLY, ROWS - EARLY), (0, EARLY)
     rp, lp, op = 2 * rx + 1 - c, 2 * lx + 1 - c, 2 * ox + 1 - c
     phase("own")
-    accumulate(tp, 0, True)
-    accumulate(tp, 1, True)
-    for half in range(2):
-        arrived(partner, half)
-        accumulate(partner, half)
+    accumulate(tp, *early, True)
+    accumulate(tp, *late, True)
+    for q in (2, 3):
+        arrived(partner, q)
+    accumulate(partner, *early)
+    for q in (0, 1):
+        arrived(partner, q)
+    accumulate(partner, *late)
     phase("near0")
+    arrived(left, 2)
+    send(left, 2, right)
+    send(left, 2, partner)
+    send(tp, 1, right)
+    arrived(right, 3)
+    send(right, 3, left)
+    send(right, 3, partner)
+    send(tp, 0, left)
+    phase("near1")
+    arrived(left, 3)
+    send(left, 3, partner)
+    arrived(right, 2)
+    send(right, 2, partner)
+    phase("near_early")
+    accumulate(left, *early)
+    accumulate(right, *early)
+    phase("near2")
     arrived(left, 0)
-    send(left, 0, right, g_send.at[6])
-    send(left, 0, partner, g_send.at[7])
+    send(left, 0, right)
+    send(left, 0, partner)
     arrived(right, 1)
-    send(right, 1, left, g_send.at[8])
-    send(right, 1, partner, g_send.at[9])
-    phase("near0_acc")
-    accumulate(left, 0)
-    accumulate(right, 1)
-    arrived(lp, 0)
-    accumulate(lp, 0)
-    arrived(rp, 1)
-    accumulate(rp, 1)
-    phase("near1")
-    arrived(left, 1)
-    send(left, 1, partner, g_send.at[10])
-    arrived(right, 0)
-    send(right, 0, partner, g_send.at[11])
-    phase("near1_acc")
-    accumulate(left, 1)
-    accumulate(right, 0)
-    arrived(lp, 1)
-    accumulate(lp, 1)
-    arrived(rp, 0)
-    accumulate(rp, 0)
-    phase("far")
-    arrived(opp, 0)
-    send(opp, 0, partner, g_send.at[12])
-    arrived(opp, 1)
-    send(opp, 1, partner, g_send.at[13])
-    phase("far_acc")
-    accumulate(opp, 0)
-    accumulate(opp, 1)
-    phase("far_p")
-    for half in range(2):
-        arrived(op, half)
-        accumulate(op, half)
+    send(right, 1, left)
+    send(right, 1, partner)
+    phase("nearp_early")
+    for src in (lp, rp):
+        arrived(src, 2)
+        arrived(src, 3)
+        accumulate(src, *early)
+    phase("far_early")
+    for q in (2, 3):
+        arrived(opp, q)
+        send(opp, q, partner)
+    accumulate(opp, *early)
+    phase("farp_early")
+    for q in (2, 3):
+        arrived(op, q)
+    accumulate(op, *early)
 
     phase("edge")
     edge_s[...] = acc[ROWS - 16 : ROWS, 0:CONV].astype(BF16)
     edge = remote(edge_s, edge_r, e_sem.at[0], e_sem.at[1], seq=nxt)
     edge.start()
-    mx[8 : 8 + ROWS, :] = acc[:, 0:CONV].astype(BF16).astype(F32)
-
-    phase("steps")
+    mx[8 + EARLY : 8 + ROWS, :] = acc[EARLY:ROWS, 0:CONV].astype(BF16).astype(F32)
+
     tri = (
         lax.broadcasted_iota(jnp.int32, (GROUP, GROUP), 0) >= lax.broadcasted_iota(jnp.int32, (GROUP, GROUP), 1)
     ).astype(F32)
-    for b in range(2):
+
+    def steps(b):
         rr = slice(b * GROUP, (b + 1) * GROUP)
         raw = acc[rr, CONV:WIDE] + small[0:1, :]
         dt = jnp.maximum(raw, 0.0) + jnp.log1p(jnp.exp(-jnp.abs(raw)))
@@ -222,20 +231,8 @@
         )
         cum_s[rr, :] = cum
         dt_s[rr, :] = dt
-    ends = jnp.concatenate([cum_s[GROUP - 1 : GROUP, :], cum_s[ROWS - 1 : ROWS, :]], axis=0)
-    total = ends[0:1, :] + ends[1:2, :]
-    row8 = lax.broadcasted_iota(jnp.int32, (8, ST), 0)
-    t_send[...] = jnp.where(row8 == z, total, 0.0)
-
-    def tcopy(k):
-        return remote(t_send, t_recv.at[z], ts_sem.at[k], tr_sem.at[z], seq=y * 8 + (z + k) % 8)
-
-    for k in range(1, 8):
-        tcopy(k).start()
-        sent.append(tcopy(k))
-    t_recv[z] = t_send[...]
-
-    def conv(b):
+
+    def conv(b, first=0, last=CONV // 128 - 1):
         def body(j, carry):
             cols = pl.ds(pl.multiple_of(j * 128, 128), 128)
 
@@ -248,7 +245,7 @@
             act[pl.ds(b * GROUP, GROUP), cols] = taps(kern, cols)
             return carry
 
-        lax.fori_loop(0, CONV // 128, body, 0)
+        lax.fori_loop(first, last, body, 0)
 
     loads[4].wait()
     loads[5].wait()
@@ -261,11 +258,48 @@
         inject_t = act[rr, CH : CH + ST].astype(F32).T.astype(BF16)
         return dot(inject_t, scaled)
 
+    phase("steps1")
+    steps(1)
     phase("conv1")
     conv(1)
+    phase("near3")
+    arrived(left, 1)
+    send(left, 1, partner)
+    arrived(right, 0)
+    send(right, 0, partner)
+    accumulate(left, *late)
+    accumulate(right, *late)
     phase("contrib1")
-    c1 = contribution(1)
-    st_f[...] = c1
+    st_f[...] = contribution(1)
+    phase("far_late")
+    for q in (0, 1):
+        arrived(opp, q)
+        send(opp, q, partner)
+    for src in (lp, rp):
+        arrived(src, 0)
+        arrived(src, 1)
+        accumulate(src, *late)
+    accumulate(opp, *late)
+    phase("farp_late")
+    for q in (0, 1):
+        arrived(op, q)
+    accumulate(op, *late)
+    mx[8 : 8 + EARLY, :] = acc[0:EARLY, 0:CONV].astype(BF16).astype(F32)
+    phase("steps0")
+    steps(0)
+    ends = jnp.concatenate([cum_s[GROUP - 1 : GROUP, :], cum_s[ROWS - 1 : ROWS, :]], axis=0)
+    total = ends[0:1, :] + ends[1:2, :]
+    row8 = lax.broadcasted_iota(jnp.int32, (8, ST), 0)
+    t_send[...] = jnp.where(row8 == z, total, 0.0)
+
+    def tcopy(k):
+        return remote(t_send, t_recv.at[z], ts_sem.at[k], tr_sem.at[z], seq=y * 8 + (z + k) % 8)
+
+    for k in range(1, 8):
+        tcopy(k).start()
+        sent.append(tcopy(k))
+    t_recv[z] = t_send[...]
+
     phase("edge_wait")
     edge.wait_recv()
     halo = edge_r[8:16, :].astype(F32)
@@ -289,6 +323,8 @@
     z_recv[z] = st_bf[pl.ds(pl.multiple_of(16 * z, 16), 16), :]
 
     phase("late_steps")
+    for b in range(2):
+        conv(b, CONV // 128 - 1, CONV // 128)
     for b in range(2):
         rr = slice(b * GROUP, (b + 1) * GROUP)
         cumt_s[b] = (cum_s[rr, :] * LOG2E).T[0:16, :]
@@ -331,66 +367,76 @@
     phase("intra")
     lax.fori_loop(0, 2, intra_body, 0)
 
-    phase("zwait")
+    phase("decays")
     for k in range(1, 8):
         src = (z + k) % 8
-        remote(st_bf.at[0:16, :], z_recv.at[src], zs_sem.at[k], zr_sem.at[src], seq=prv).wait_recv()
         remote(t_send, t_recv.at[src], ts_sem.at[k], tr_sem.at[src], seq=prv).wait_recv()
-    phase("prefix")
     tall = t_recv[0]
     for k in range(1, 8):
         tall = tall + t_recv[k]
     texp = expanded(jnp.exp(tall))
-    prefix = jnp.zeros((16, CH), F32)
     tsum = jnp.zeros((1, ST), F32)
     tpre = []
     for k in range(8):
-        f_pre = prefix
-        pref[16 * k : 16 * (k + 1), 0:CH] = f_pre
         tpre.append(tsum)
-        prefix = texp[k : k + 1, :] * prefix + z_recv[k].astype(F32)
         tsum = tsum + tall[k : k + 1, :]
-    y_send[...] = prefix.astype(BF16)
+    pexp = expanded(jnp.exp(jnp.concatenate(tpre, axis=0)))
     yt_send[...] = jnp.where(row8 == y, tsum, 0.0)
     for k in range(1, 4):
         to = ((y + k) % 4) * 8 + z
-        a = remote(y_send, y_recv.at[y], ys_sem.at[k], yr_sem.at[y], seq=to)
-        b = remote(yt_send, yt_recv.at[y], yts_sem.at[k], ytr_sem.at[y], seq=to)
-        for copy in (a, b):
-            copy.start()
-            sent.append(copy)
-    y_recv[y] = y_send[...]
+        copy = remote(yt_send, yt_recv.at[y], yts_sem.at[k], ytr_sem.at[y], seq=to)
+        copy.start()
+        sent.append(copy)
     yt_recv[y] = yt_send[...]
 
-    phase("gate")
+    phase("gate0")
     loads[10].wait()
 
-    def gate_body(half, carry):
-        rr = pl.ds(pl.multiple_of(half * GROUP, GROUP), GROUP)
+    def gate_half(half):
+        rr = slice(half * GROUP, (half + 1) * GROUP)
         v = dot(xb[0, rr, :], wg[0:KD, :])
         for src in range(1, 8):
             v = v + dot(xb[src, rr, :], wg[src * KD : (src + 1) * KD, :])
         acc_g[rr, :] = silu(v.astype(BF16).astype(F32))
-        return carry
-
-    lax.fori_loop(0, 2, gate_body, 0)
+
+    gate_half(0)
+
+    phase("zwait")
+    for k in range(1, 8):
+        src = (z + k) % 8
+        remote(st_bf.at[0:16, :], z_recv.at[src], zs_sem.at[k], zr_sem.at[src], seq=prv).wait_recv()
+    phase("prefix")
+    prefix = jnp.zeros((16, CH), F32)
+    for k in range(8):
+        pref[16 * k : 16 * (k + 1), 0:CH] = prefix
+        prefix = texp[k : k + 1, :] * prefix + z_recv[k].astype(F32)
+    y_send[...] = prefix.astype(BF16)
+    for k in (2, 1, 3):
+        to = ((y + k) % 4) * 8 + z
+        copy = remote(y_send, y_recv.at[y], ys_sem.at[k], yr_sem.at[y], seq=to)
+        copy.start()
+        sent.append(copy)
+    y_recv[y] = y_send[...]
+
+    phase("gate1")
+    gate_half(1)
     phase("ywait")
-
     for k in range(1, 4):
         src = (y + k) % 4
-        remote(y_send, y_recv.at[src], ys_sem.at[k], yr_sem.at[src], seq=prv).wait_recv()
         remote(yt_send, yt_recv.at[src], yts_sem.at[k], ytr_sem.at[src], seq=prv).wait_recv()
-    phase("ycomb")
     yall = yt_recv[0]
     for k in range(1, 4):
         yall = yall + yt_recv[k]
     yexp = expanded(jnp.exp(yall))
+    for k in range(1, 4):
+        src = (y + k) % 4
+        remote(y_send, y_recv.at[src], ys_sem.at[k], yr_sem.at[src], seq=prv).wait_recv()
+    phase("ycomb")
     run = jnp.zeros((16, CH), F32)
     chosen = run
     for k in range(3):
         run = yexp[k : k + 1, :] * run + y_recv[k].astype(F32)
         chosen = jnp.where(y == k + 1, run, chosen)
-    pexp = expanded(jnp.exp(jnp.concatenate(tpre, axis=0)))
     for k in range(8):
         f_send[k] = (pref[16 * k : 16 * (k + 1), 0:CH] + pexp[k : k + 1, :] * chosen).astype(BF16)
     mine = pl.ds(pl.multiple_of(16 * z, 16), 16)
@@ -541,7 +587,7 @@
         vm((4, NQ, 64, QC), F32), vm((4, NQ, 64, QC), BF16), vm((4, NQ, 64, QC), BF16),
         vm((3, NQ, 64, QC), BF16), vm((NQ, 64, QC), BF16),
         vm((NQ, 64, QC), BF16), vm((NQ, 64, QC), BF16), vm((128, 128), F32),
-        dma((12,)), dma((14,)), dma((8, 2)), dma((2,)), dma((8,)), dma((8,)), dma((8,)), dma((8,)),
+        dma((12,)), dma((28,)), dma((8, 4)), dma((2,)), dma((8,)), dma((8,)), dma((8,)), dma((8,)),
         dma((4,)), dma((4,)), dma((4,)), dma((4,)), dma((8,)), dma((8,)),
         dma((8,)), dma((8,)), dma((4, NQ)), dma((4, NQ)), dma((NQ, 3)), dma((NQ, 3)),
     ]
@@ -550,7 +596,7 @@
     return pl.pallas_call(
         kernel,
         name="layer",
-        out_shape=jax.ShapeDtypeStruct((ROWS // 8, D), BF16),
+        out_shape=pltpu.VMEM((ROWS // 8, D), BF16),
         in_specs=[hbm] * 12,
         out_specs=local,
         scratch_shapes=scratch,

time: 66.8 us -> 62.9 us (0.942)
  Pallas kernels: 64.9 us -> 62.1 us
  local copies, waits for them, and re-layouts: 1.72 us -> 0.73 us
    pallas_call x1, Pallas kernels: 64.9 us -> 62.1 us  [on_device(): pl.pallas_call(kernel, name='layer', out_shape=pltpu.VMEM((ROWS // 8, D),...]
    unnamed x1, local copies, waits for them, and re-layouts: 1.72 us -> 0.73 us
where the time goes in v3:
time: 62.9 us; the launch traced here: 62.8 us
  Pallas kernels  62.1 us (99%)
  local copies, waits for them, and re-layouts  0.73 us (1%)
    pallas_call x1, Pallas kernels, on_device(): pl.pallas_call(kernel, name='layer', out_shape=pltpu.VMEM((ROWS // 8, D),...  62.1 us

profile of v3, /device:TPU:1, one launch (start us, length us, event | category | flops | bytes accessed | tf_op | source)
XLA Modules:
  0.0 62.8 jit_solution(11773633266689667797)
XLA Ops:
  0.0 62.1 %layer.1 = bf16[64,2560]{1,0:T(8,128)(2,1)S(1)} custom-call(bf16[320,512]{1,0:T(8,128)(2,1)} %bitcast.5, bf16[2560,640]{1,0:T(8,128)(2,1)} %w_gate.1, bf16[2560,640]{1,0:T(8,128)(2,1)} %w_inner.1, bf16[2560,256]{1,0:T(8,128)(2,1)} %w_state.1, bf16[10,2560]{1,0:T(8,128)(2,1)} %bitcast.6, f32[4,640]{1,0:T(4,128)} %k_inner.1, f32[4,256]{1,0:T(4,128)} %k_state.1, ...), custom_call_target="tpu_custom_call" | custom-call | tf_op jit(solution)/shard_map/layer/pallas_call | solution.py:596
  62.1 0.7 %copy.14 = bf16[64,2560]{1,0:T(8,128)(2,1)} copy(bf16[64,2560]{1,0:T(8,128)(2,1)S(1)} %layer.1) | data formatting | bytes 655360

commit v4 on v3

--- a/solution.py
+++ b/solution.py
@@ -19,7 +19,7 @@
 WIDE = CONV + ST
 CUTS = ((0, 512), (1280, 512), (512, 768), (1792, 768))
 NQ = len(CUTS)
-PIECES = ((0, 112), (112, 128), (240, 144), (384, 128))
+PIECES = ((0, 112), (112, 128), (240, 144), (384, 128), (0, 240), (240, 272))
 EARLY = 240
 QC = 768
 LOG2E = 1.4426950408889634
@@ -64,9 +64,8 @@
     acc, acc_g, mx, act, edge_s, edge_r,
     small, expand, cum_s, dt_s, cumt_s, dtt_s,
     ssd, gexp, st_bf, st_f, c0_s, z_recv, t_send, t_recv, pref, y_send, yt_send, y_recv, yt_recv, f_send, inc, carr,
-    sq_send, sq_recv, both, keep, d_send, d_recv, r1_send, r1_recv, fin_l, fin_r, scale_s,
-    loc_sem, g_send, g_recv, e_sem, zs_sem, zr_sem, ts_sem, tr_sem, ys_sem, yr_sem, yts_sem, ytr_sem, fs_sem, fr_sem,
-    qs_sem, qr_sem, ds_sem, dr_sem, rs_sem, rr_sem,
+    sq_send, sq_recv, g_rows, both, keep, d_send, d_recv, r1_send, r1_recv, fin, e_send, e_recv, scale_s,
+    loc_sem, g_send, g_near, g_pair, e_sem, t_sem, z_sem, yt_sem, y_sem, f_sem, q_sem, ds_sem, dr_sem, rs_sem, rr_sem,
 ):
     seq = lax.axis_index("seq")
     tp = lax.axis_index("tp")
@@ -87,13 +86,15 @@
     phase = Phases()
     phase("start")
     copies = (
-        (tok, tok_t), (w_inner, wall.at[:, 0:CH]), (w_state, wall.at[:, CH:CONV]), (w_step, step_t),
-        (k_inner, kern.at[:, 0:CH]), (k_state, kern.at[:, CH:CONV]), (bias, vec.at[0:1]), (rate, vec.at[1:2]),
-        (skip, vec.at[2:3]), (gain, gain_v), (w_gate, wg), (w_out, wo),
+        (tok, tok_t, 0), (w_inner, wall.at[:, 0:CH], 1), (w_state, wall.at[:, CH:CONV], 1), (w_step, step_t, 2),
+        (bias, vec.at[0:1], 3), (rate, vec.at[1:2], 3), (skip, vec.at[2:3], 3), (k_inner, kern.at[:, 0:CH], 4),
+        (k_state, kern.at[:, CH:CONV], 4), (gain, gain_v, 5), (w_gate, wg, 6), (w_out, wo, 7),
     )
-    loads = [pltpu.make_async_copy(src, dst, loc_sem.at[i]) for i, (src, dst) in enumerate(copies)]
-    for load in loads:
-        load.start()
+    for src, dst, i in copies:
+        pltpu.make_async_copy(src, dst, loc_sem.at[i]).start()
+
+    def loaded(ref, i):
+        pltpu.make_async_copy(ref, ref, loc_sem.at[i]).wait()
 
     barrier = pltpu.get_barrier_semaphore()
     for k in range(1, 8):
@@ -116,45 +117,41 @@
         return dot(hi, expand[...]) + dot(lo, expand[...])
 
     phase("turn")
-    loads[0].wait()
+    loaded(tok_t, 0)
     xb[tp] = tok_t[...].T
     phase("barrier")
     pl.semaphore_wait(barrier, 19)
 
     phase("send")
-    sent = []
-
-    def piece(src, q, to, ssem):
+    def piece(src, q, to, sem):
         start, rows = PIECES[q]
         part = xb.at[src, pl.ds(start, rows), :]
-        return remote(part, part, ssem, g_recv.at[src, q], tp=to)
-
-    gathered = []
-
-    def send(src, q, to):
-        copy = piece(src, q, to, g_send.at[len(gathered)])
-        copy.start()
-        gathered.append(copy)
-        sent.append(copy)
-
-    def arrived(src, q):
-        piece(src, q, partner, g_send.at[0]).wait_recv()
-
-    for a, b in ((2, 3), (3, 2), (0, 1)):
-        send(tp, a, right)
-        send(tp, b, left)
-    for q in (2, 3, 0, 1):
-        send(tp, q, partner)
+        return remote(part, part, g_send.at[0], sem, tp=to)
+
+    def send(src, q, to, origin):
+        piece(src, q, to, g_pair.at[origin, int(q in (2, 3, 5))] if to is partner else g_near.at[origin, q]).start()
+
+    def arrived(src, q, origin):
+        piece(src, q, partner, g_near.at[origin, q]).wait_recv()
+
+    def pair_arrived(src, rows, origin):
+        part = xb.at[src, pl.ds(rows[0], rows[1]), :]
+        remote(part, part, g_send.at[0], g_pair.at[origin, 1 if rows[0] else 0], tp=partner).wait_recv()
+
+    for a, b in ((2, 3), (3, 2), (4, 4)):
+        send(tp, a, right, 0)
+        send(tp, b, left, 1)
+    for q in (5, 4):
+        send(tp, q, partner, 3)
     phase("step_turn")
-    loads[3].wait()
+    loaded(step_t, 2)
     step_f[...] = jnp.zeros_like(step_f)
     step_f[0:HD, :] = step_t[...].astype(F32)
     wall[:, CONV:WIDE] = step_f[...].T.astype(BF16)
-    for i in (6, 7, 8):
-        loads[i].wait()
-        small[8 * (i - 6) : 8 * (i - 6) + 1, 0:HD] = vec[i - 6 : i - 5, :]
-    loads[1].wait()
-    loads[2].wait()
+    loaded(vec, 3)
+    for i in range(3):
+        small[8 * i : 8 * i + 1, 0:HD] = vec[i : i + 1, :]
+    loaded(wall.at[:, 0:CONV], 1)
 
     def accumulate(src, start, rows, first=False):
         rr = pl.ds(start, rows)
@@ -166,49 +163,52 @@
     phase("own")
     accumulate(tp, *early, True)
     accumulate(tp, *late, True)
-    for q in (2, 3):
-        arrived(partner, q)
+    pair_arrived(partner, early, 3)
     accumulate(partner, *early)
-    for q in (0, 1):
-        arrived(partner, q)
+    pair_arrived(partner, late, 3)
     accumulate(partner, *late)
     phase("near0")
-    arrived(left, 2)
-    send(left, 2, right)
-    send(left, 2, partner)
-    send(tp, 1, right)
-    arrived(right, 3)
-    send(right, 3, left)
-    send(right, 3, partner)
-    send(tp, 0, left)
+    arrived(left, 2, 0)
+    send(left, 2, right, 2)
+    send(left, 2, partner, 0)
+    arrived(right, 3, 1)
+    send(right, 3, left, 2)
+    send(right, 3, partner, 1)
     phase("near1")
-    arrived(left, 3)
-    send(left, 3, partner)
-    arrived(right, 2)
-    send(right, 2, partner)
+    arrived(left, 3, 0)
+    send(left, 3, partner, 0)
+    arrived(right, 2, 1)
+    send(right, 2, partner, 1)
     phase("near_early")
     accumulate(left, *early)
     accumulate(right, *early)
+    phase("nearp_early")
+    pair_arrived(lp, early, 0)
+    accumulate(lp, *early)
+    pair_arrived(rp, early, 1)
+    accumulate(rp, *early)
     phase("near2")
-    arrived(left, 0)
-    send(left, 0, right)
-    send(left, 0, partner)
-    arrived(right, 1)
-    send(right, 1, left)
-    send(right, 1, partner)
-    phase("nearp_early")
-    for src in (lp, rp):
-        arrived(src, 2)
-        arrived(src, 3)
-        accumulate(src, *early)
+    arrived(left, 4, 0)
+    send(left, 0, right, 2)
+    send(left, 4, partner, 0)
+    arrived(right, 4, 1)
+    send(right, 1, left, 2)
+    send(right, 4, partner, 1)
+    phase("near_late")
+    accumulate(left, *late)
+    accumulate(right, *late)
+    phase("nearp_late")
+    pair_arrived(lp, late, 0)
+    accumulate(lp, *late)
+    pair_arrived(rp, late, 1)
+    accumulate(rp, *late)
     phase("far_early")
     for q in (2, 3):
-        arrived(opp, q)
-        send(opp, q, partner)
+        arrived(opp, q, 2)
+        send(opp, q, partner, 2)
     accumulate(opp, *early)
     phase("farp_early")
-    for q in (2, 3):
-        arrived(op, q)
+    pair_arrived(op, early, 2)
     accumulate(op, *early)
 
     phase("edge")
@@ -219,16 +219,16 @@
 
     tri = (
         lax.broadcasted_iota(jnp.int32, (GROUP, GROUP), 0) >= lax.broadcasted_iota(jnp.int32, (GROUP, GROUP), 1)
-    ).astype(F32)
+    ).astype(BF16)
 
     def steps(b):
         rr = slice(b * GROUP, (b + 1) * GROUP)
         raw = acc[rr, CONV:WIDE] + small[0:1, :]
         dt = jnp.maximum(raw, 0.0) + jnp.log1p(jnp.exp(-jnp.abs(raw)))
         ld = -dt * small[8:9, :]
-        cum = lax.dot_general(
-            tri, ld, (((1,), (0,)), ((), ())), precision=lax.Precision.HIGHEST, preferred_element_type=F32
-        )
+        hi = ld.astype(BF16)
+        mid, low = split2(ld - hi.astype(F32))
+        cum = dot(tri, hi) + dot(tri, mid) + dot(tri, low)
         cum_s[rr, :] = cum
         dt_s[rr, :] = dt
 
@@ -247,8 +247,7 @@
 
         lax.fori_loop(first, last, body, 0)
 
-    loads[4].wait()
-    loads[5].wait()
+    loaded(kern, 4)
 
     def contribution(b):
         rr = slice(b * GROUP, (b + 1) * GROUP)
@@ -260,29 +259,18 @@
 
     phase("steps1")
     steps(1)
+    phase("far_late")
+    for q in (0, 1):
+        arrived(opp, q, 2)
+        send(opp, q, partner, 2)
     phase("conv1")
     conv(1)
-    phase("near3")
-    arrived(left, 1)
-    send(left, 1, partner)
-    arrived(right, 0)
-    send(right, 0, partner)
-    accumulate(left, *late)
-    accumulate(right, *late)
     phase("contrib1")
     st_f[...] = contribution(1)
-    phase("far_late")
-    for q in (0, 1):
-        arrived(opp, q)
-        send(opp, q, partner)
-    for src in (lp, rp):
-        arrived(src, 0)
-        arrived(src, 1)
-        accumulate(src, *late)
+    phase("far_acc")
     accumulate(opp, *late)
     phase("farp_late")
-    for q in (0, 1):
-        arrived(op, q)
+    pair_arrived(op, late, 2)
     accumulate(op, *late)
     mx[8 : 8 + EARLY, :] = acc[0:EARLY, 0:CONV].astype(BF16).astype(F32)
     phase("steps0")
@@ -292,12 +280,8 @@
     row8 = lax.broadcasted_iota(jnp.int32, (8, ST), 0)
     t_send[...] = jnp.where(row8 == z, total, 0.0)
 
-    def tcopy(k):
-        return remote(t_send, t_recv.at[z], ts_sem.at[k], tr_sem.at[z], seq=y * 8 + (z + k) % 8)
-
-    for k in range(1, 8):
-        tcopy(k).start()
-        sent.append(tcopy(k))
+    for k in (4, 3, 5, 2, 6, 1, 7):
+        remote(t_send, t_recv.at[z], t_sem.at[0], t_sem.at[1], seq=y * 8 + (z + k) % 8).start()
     t_recv[z] = t_send[...]
 
     phase("edge_wait")
@@ -312,14 +296,10 @@
     end_exp = expanded(jnp.exp(ends8))
     st_bf[...] = (end_exp[1:2, :] * c0_s[...] + st_f[...]).astype(BF16)
     phase("zsend")
-    def zcopy(k):
+    for k in (4, 3, 5, 2, 6, 1, 7):
         to = (z + k) % 8
-        return remote(st_bf.at[pl.ds(pl.multiple_of(16 * to, 16), 16), :], z_recv.at[z], zs_sem.at[k], zr_sem.at[z],
-                      seq=y * 8 + to)
-
-    for k in (4, 3, 5, 2, 6, 1, 7):
-        zcopy(k).start()
-        sent.append(zcopy(k))
+        part = st_bf.at[pl.ds(pl.multiple_of(16 * to, 16), 16), :]
+        remote(part, z_recv.at[z], z_sem.at[0], z_sem.at[1], seq=y * 8 + to).start()
     z_recv[z] = st_bf[pl.ds(pl.multiple_of(16 * z, 16), 16), :]
 
     phase("late_steps")
@@ -368,9 +348,13 @@
     lax.fori_loop(0, 2, intra_body, 0)
 
     phase("decays")
-    for k in range(1, 8):
-        src = (z + k) % 8
-        remote(t_send, t_recv.at[src], ts_sem.at[k], tr_sem.at[src], seq=prv).wait_recv()
+    def all_arrived(ref, sem):
+        remote(ref, ref, sem.at[0], sem.at[1], seq=prv).wait_recv()
+
+    def all_sent(ref, sem):
+        remote(ref, ref, sem, sem, seq=prv).wait_send()
+
+    all_arrived(t_recv.at[0:7], t_sem)
     tall = t_recv[0]
     for k in range(1, 8):
         tall = tall + t_recv[k]
@@ -384,27 +368,11 @@
     yt_send[...] = jnp.where(row8 == y, tsum, 0.0)
     for k in range(1, 4):
         to = ((y + k) % 4) * 8 + z
-        copy = remote(yt_send, yt_recv.at[y], yts_sem.at[k], ytr_sem.at[y], seq=to)
-        copy.start()
-        sent.append(copy)
+        remote(yt_send, yt_recv.at[y], yt_sem.at[0], yt_sem.at[1], seq=to).start()
     yt_recv[y] = yt_send[...]
 
-    phase("gate0")
-    loads[10].wait()
-
-    def gate_half(half):
-        rr = slice(half * GROUP, (half + 1) * GROUP)
-        v = dot(xb[0, rr, :], wg[0:KD, :])
-        for src in range(1, 8):
-            v = v + dot(xb[src, rr, :], wg[src * KD : (src + 1) * KD, :])
-        acc_g[rr, :] = silu(v.astype(BF16).astype(F32))
-
-    gate_half(0)
-
     phase("zwait")
-    for k in range(1, 8):
-        src = (z + k) % 8
-        remote(st_bf.at[0:16, :], z_recv.at[src], zs_sem.at[k], zr_sem.at[src], seq=prv).wait_recv()
+    all_arrived(z_recv.at[0:7], z_sem)
     phase("prefix")
     prefix = jnp.zeros((16, CH), F32)
     for k in range(8):
@@ -413,24 +381,27 @@
     y_send[...] = prefix.astype(BF16)
     for k in (2, 1, 3):
         to = ((y + k) % 4) * 8 + z
-        copy = remote(y_send, y_recv.at[y], ys_sem.at[k], yr_sem.at[y], seq=to)
-        copy.start()
-        sent.append(copy)
+        remote(y_send, y_recv.at[y], y_sem.at[0], y_sem.at[1], seq=to).start()
     y_recv[y] = y_send[...]
 
     phase("gate1")
+    loaded(wg, 6)
+
+    def gate_half(half):
+        rr = slice(half * GROUP, (half + 1) * GROUP)
+        v = dot(xb[0, rr, :], wg[0:KD, :])
+        for src in range(1, 8):
+            v = v + dot(xb[src, rr, :], wg[src * KD : (src + 1) * KD, :])
+        acc_g[rr, :] = silu(v.astype(BF16).astype(F32))
+
     gate_half(1)
     phase("ywait")
-    for k in range(1, 4):
-        src = (y + k) % 4
-        remote(yt_send, yt_recv.at[src], yts_sem.at[k], ytr_sem.at[src], seq=prv).wait_recv()
+    all_arrived(yt_recv.at[0:3], yt_sem)
     yall = yt_recv[0]
     for k in range(1, 4):
         yall = yall + yt_recv[k]
     yexp = expanded(jnp.exp(yall))
-    for k in range(1, 4):
-        src = (y + k) % 4
-        remote(y_send, y_recv.at[src], ys_sem.at[k], yr_sem.at[src], seq=prv).wait_recv()
+    all_arrived(y_recv.at[0:3], y_sem)
     phase("ycomb")
     run = jnp.zeros((16, CH), F32)
     chosen = run
@@ -442,22 +413,19 @@
     mine = pl.ds(pl.multiple_of(16 * z, 16), 16)
     for k in (4, 3, 5, 2, 6, 1, 7):
         to = (z + k) % 8
-        copy = remote(f_send.at[to], inc.at[mine, :], fs_sem.at[k], fr_sem.at[z], seq=y * 8 + to)
-        copy.start()
-        sent.append(copy)
+        remote(f_send.at[to], inc.at[mine, :], f_sem.at[0], f_sem.at[1], seq=y * 8 + to).start()
     inc[mine, :] = f_send[z]
 
     phase("skip")
+    phase("gate0")
+    gate_half(0)
     skips = expanded(small[16:24, :])[0:1, :]
     ssd[...] = ssd[...] + skips * act[:, 0:CH].astype(F32)
-    loads[9].wait()
-    loads[11].wait()
+    loaded(gain_v, 5)
+    loaded(wo, 7)
     phase("fwait")
 
-    for k in range(1, 8):
-        src = (z + k) % 8
-        there = pl.ds(pl.multiple_of(16 * src, 16), 16)
-        remote(f_send.at[0], inc.at[there, :], fs_sem.at[k], fr_sem.at[src], seq=prv).wait_recv()
+    all_arrived(inc.at[0:112, :], f_sem)
     phase("gated")
     carr[0] = inc[...]
     carr[1] = (c0_s[...] + end_exp[0:1, :] * inc[...].astype(F32)).astype(BF16)
@@ -465,90 +433,107 @@
     ones = jnp.ones((8, CH), BF16)
     gain_row = gain_v[...].reshape(1, CH)
 
-    def gate(chip):
+    def gate(j, chip):
         rr = pl.ds(pl.multiple_of(chip * 128, 128), 128)
         reads = dot(act[rr, CH + ST : CONV], carr[chip // 2])
         g = (ssd[rr, :] + reads * gexp[rr, :]) * acc_g[rr, :]
         hi, lo = split2(g * g)
         sq_send[chip] = dot_nt(ones, hi) + dot_nt(ones, lo)
-        return (g * gain_row).astype(BF16)
-
-    def started(copy):
-        copy.start()
-        sent.append(copy)
+        g_rows[j] = (g * gain_row).astype(BF16)
+
+    def d_slot(j, q):
+        return q if j == 0 else 8 if j == 3 else 2 + 2 * j + q % 2
 
     def part(ref, *at):
         return ref.at[at + (slice(None), pl.ds(0, CUTS[at[-1]][1]))]
 
     def dcopy(j, q):
-        return remote(part(d_send, j, q), part(d_recv, j, q), ds_sem.at[j, q], dr_sem.at[j, q], tp=partner)
-
-    def project(j, rows):
-        for q, (start, width) in enumerate(CUTS):
+        return remote(part(d_send, j, q), part(d_recv, j, q), ds_sem.at[0], dr_sem.at[d_slot(j, q)], tp=partner)
+
+    def project(j, which=range(NQ)):
+        for q in which:
+            start, width = CUTS[q]
             cols = pl.ds(0, width)
-            v = dot(rows, wo[:, start : start + width])
+            v = dot(g_rows[j], wo[:, start : start + width])
             both[0, :, cols] = v[0:64, :]
             both[1, :, cols] = v[64:128, :]
             d_send[j, q, :, cols] = both[1 - c, :, cols].astype(BF16)
-            started(dcopy(j, q))
+            dcopy(j, q).start()
             keep[j, q, :, cols] = both[c, :, cols]
 
     def paired(j, q):
-        dcopy(j, q).wait_recv()
+        if j == 0:
+            dcopy(j, q).wait_recv()
+        elif q < 2 and (j < 3 or q == 0):
+            ref = wo.at[0:64, 0 : D if j == 3 else D // 2]
+            remote(ref, ref, ds_sem.at[0], dr_sem.at[d_slot(j, q)], tp=partner).wait_recv()
         cols = pl.ds(0, CUTS[q][1])
         return keep[j, q, :, cols] + d_recv[j, q, :, cols].astype(F32)
 
     def hop1(q):
         to = right if q % 2 == 0 else left
-        return remote(part(r1_send, 0, q), part(r1_recv, q), rs_sem.at[q, 0], rr_sem.at[q, 0], tp=to)
-
-    def direct(q):
-        if q % 2 == 0:
-            return remote(part(r1_send, 1, q), part(fin_r, q), rs_sem.at[q, 1], rr_sem.at[q, 1], tp=left)
-        return remote(part(r1_send, 1, q), part(fin_l, q), rs_sem.at[q, 1], rr_sem.at[q, 1], tp=right)
+        return remote(part(r1_send, 0, q), part(r1_recv, q), rs_sem.at[0], rr_sem.at[q], tp=to)
+
+    def direct(way):
+        to = left if way == 0 else right
+        return remote(e_send.at[way], e_recv.at[way], rs_sem.at[0], rr_sem.at[NQ + way], tp=to)
 
     def hop2(q):
-        if q % 2 == 0:
-            return remote(part(r1_send, 2, q), part(fin_l, q), rs_sem.at[q, 2], rr_sem.at[q, 2], tp=right)
-        return remote(part(r1_send, 2, q), part(fin_r, q), rs_sem.at[q, 2], rr_sem.at[q, 2], tp=left)
+        to = right if q % 2 == 0 else left
+        return remote(part(r1_send, 1, q), part(fin, q), rs_sem.at[0], rr_sem.at[NQ + 2 + q], tp=to)
+
+    def within(q):
+        start, width = CUTS[q]
+        return pl.ds(start % (D // 2), width)
 
     def put(which, q, value):
         r1_send[which, q, :, pl.ds(0, CUTS[q][1])] = value.astype(BF16)
 
-    project(0, gate(ox))
+    def hop1_start(q):
+        put(0, q, paired(0, q))
+        hop1(q).start()
+
+    gate(0, ox)
+    project(0)
+    phase("hop1")
+    hop1_start(0)
+    hop1_start(1)
     phase("block1")
-    rows = gate(lx)
-    phase("hop1")
-    for q in range(NQ):
-        put(0, q, paired(0, q))
-        started(hop1(q))
-    phase("block1_mm")
-    project(1, rows)
-    phase("block2")
-    project(2, gate(rx))
-    phase("direct")
-    for q in range(NQ):
-        put(1, q, paired(1 if q % 2 == 0 else 2, q))
-        started(direct(q))
-    phase("block3")
-    project(3, gate(x))
+    gate(1, lx)
+    phase("hop1b")
+    hop1_start(2)
+    hop1_start(3)
+    phase("block12")
+    project(1, (0, 2))
+    gate(2, rx)
+    project(2, (1, 3))
+    gate(3, x)
     for k in range(1, 8):
         to = (tp + k) % 8
-        started(remote(sq_send.at[to // 2], sq_recv.at[tp], qs_sem.at[k], qr_sem.at[tp], tp=to))
+        remote(sq_send.at[to // 2], sq_recv.at[tp], q_sem.at[0], q_sem.at[1], tp=to).start()
     sq_recv[tp] = sq_send[x]
+    phase("block12b")
+    project(1, (1, 3))
+    phase("direct")
+    for q in (0, 2, 1, 3):
+        e_send[q % 2, :, within(q)] = paired(1 if q % 2 == 0 else 2, q).astype(BF16)
+        if q >= 2:
+            direct(q % 2).start()
+    phase("block23")
+    project(2, (0, 2))
+    project(3)
     phase("hop2")
     for q in range(NQ):
         v = paired(2 if q % 2 == 0 else 1, q)
         hop1(q).wait_recv()
-        put(2, q, v + r1_recv[q, :, pl.ds(0, CUTS[q][1])].astype(F32))
-        started(hop2(q))
+        put(1, q, v + r1_recv[q, :, pl.ds(0, CUTS[q][1])].astype(F32))
+        hop2(q).start()
     phase("own_sum")
     for q in range(NQ):
         keep[3, q, :, pl.ds(0, CUTS[q][1])] = paired(3, q)
     phase("scale")
-    for k in range(1, 8):
-        src = (tp + k) % 8
-        remote(sq_send.at[0], sq_recv.at[src], qs_sem.at[k], qr_sem.at[src], tp=partner).wait_recv()
+    tiles = sq_recv.at[0:7]
+    remote(tiles, tiles, q_sem.at[0], q_sem.at[1], tp=partner).wait_recv()
     sq = sq_recv[0]
     for k in range(1, 8):
         sq = sq + sq_recv[k]
@@ -556,16 +541,23 @@
     scale_s[...] = jnp.broadcast_to(factor[0:1, :], (128, 128)).T
     scale = scale_s[pl.ds(pl.multiple_of(64 * c, 64), 64), :]
     for q, (start, width) in enumerate(CUTS):
-        direct(q).wait_recv()
+        if q < 2:
+            direct(q).wait_recv()
         hop2(q).wait_recv()
+        shift = start % (D // 2)
         for j in range(width // 128):
             cols = slice(j * 128, (j + 1) * 128)
-            v = keep[3, q, :, cols] + fin_l[q, :, cols].astype(F32) + fin_r[q, :, cols].astype(F32)
+            more = slice(shift + j * 128, shift + (j + 1) * 128)
+            v = keep[3, q, :, cols] + fin[q, :, cols].astype(F32) + e_recv[q % 2, :, more].astype(F32)
             out[:, start + j * 128 : start + (j + 1) * 128] = (v * scale).astype(BF16)
     phase("drain")
     edge.wait_send()
-    for copy in sent:
-        copy.wait_send()
+    for ref, sem in (
+        (xb.at[0:7], g_send), (t_recv.at[0:7], t_sem), (z_recv.at[0:7], z_sem), (yt_recv.at[0:3], yt_sem),
+        (y_recv.at[0:3], y_sem), (f_send.at[0:7], f_sem), (sq_recv.at[0:7], q_sem),
+        (wo.at[0:256, :], ds_sem), (wo.at[0:192, :], rs_sem),
+    ):
+        all_sent(ref, sem.at[0])
     phase.close()
 
 
@@ -583,13 +575,12 @@
         vm((8, 16, CH), BF16), vm((8, ST), F32), vm((8, 8, ST), F32), vm((ST, CONV), F32),
         vm((16, CH), BF16), vm((8, ST), F32), vm((4, 16, CH), BF16), vm((4, 8, ST), F32),
         vm((8, 16, CH), BF16), vm((ST, CH), BF16), vm((2, ST, CH), BF16),
-        vm((4, 8, ST), F32), vm((8, 8, ST), F32), vm((2, 64, QC), F32),
+        vm((4, 8, ST), F32), vm((8, 8, ST), F32), vm((4, ST, CH), BF16), vm((2, 64, QC), F32),
         vm((4, NQ, 64, QC), F32), vm((4, NQ, 64, QC), BF16), vm((4, NQ, 64, QC), BF16),
-        vm((3, NQ, 64, QC), BF16), vm((NQ, 64, QC), BF16),
-        vm((NQ, 64, QC), BF16), vm((NQ, 64, QC), BF16), vm((128, 128), F32),
-        dma((12,)), dma((28,)), dma((8, 4)), dma((2,)), dma((8,)), dma((8,)), dma((8,)), dma((8,)),
-        dma((4,)), dma((4,)), dma((4,)), dma((4,)), dma((8,)), dma((8,)),
-        dma((8,)), dma((8,)), dma((4, NQ)), dma((4, NQ)), dma((NQ, 3)), dma((NQ, 3)),
+        vm((2, NQ, 64, QC), BF16), vm((NQ, 64, QC), BF16), vm((NQ, 64, QC), BF16),
+        vm((2, 64, D // 2), BF16), vm((2, 64, D // 2), BF16), vm((128, 128), F32),
+        dma((8,)), dma((1,)), dma((3, 5)), dma((4, 2)), dma((2,)), dma((2,)), dma((2,)), dma((2,)), dma((2,)), dma((2,)),
+        dma((2,)), dma((1,)), dma((9,)), dma((1,)), dma((2 * NQ + 2,)),
     ]
     hbm = pl.BlockSpec(memory_space=pl.ANY)
     local = pl.BlockSpec(memory_space=pltpu.VMEM)

time: 62.9 us -> 61.7 us (0.981)
  Pallas kernels: 62.1 us -> 60.9 us
    pallas_call x1, Pallas kernels: 62.1 us -> 60.9 us  [on_device(): pl.pallas_call(kernel, name='layer', out_shape=pltpu.VMEM((ROWS // 8, D),...]
where the time goes in v4:
time: 61.7 us; the launch traced here: 61.6 us
  Pallas kernels  60.9 us (99%)
  local copies, waits for them, and re-layouts  0.73 us (1%)
    pallas_call x1, Pallas kernels, on_device(): pl.pallas_call(kernel, name='layer', out_shape=pltpu.VMEM((ROWS // 8, D),...  60.9 us

profile of v4, /device:TPU:1, one launch (start us, length us, event | category | flops | bytes accessed | tf_op | source)
XLA Modules:
  0.0 61.6 jit_solution(6271008541227719564)
XLA Ops:
  0.0 60.9 %layer.1 = bf16[64,2560]{1,0:T(8,128)(2,1)S(1)} custom-call(bf16[320,512]{1,0:T(8,128)(2,1)} %bitcast.5, bf16[2560,640]{1,0:T(8,128)(2,1)} %w_gate.1, bf16[2560,640]{1,0:T(8,128)(2,1)} %w_inner.1, bf16[2560,256]{1,0:T(8,128)(2,1)} %w_state.1, bf16[10,2560]{1,0:T(8,128)(2,1)} %bitcast.6, f32[4,640]{1,0:T(4,128)} %k_inner.1, f32[4,256]{1,0:T(4,128)} %k_state.1, ...), custom_call_target="tpu_custom_call" | custom-call | tf_op jit(solution)/shard_map/layer/pallas_call | solution.py:587
  60.9 0.7 %copy.14 = bf16[64,2560]{1,0:T(8,128)(2,1)} copy(bf16[64,2560]{1,0:T(8,128)(2,1)S(1)} %layer.1) | data formatting | bytes 655360

commit v5 on v4

--- a/solution.py
+++ b/solution.py
@@ -85,17 +85,6 @@
 
     phase = Phases()
     phase("start")
-    copies = (
-        (tok, tok_t, 0), (w_inner, wall.at[:, 0:CH], 1), (w_state, wall.at[:, CH:CONV], 1), (w_step, step_t, 2),
-        (bias, vec.at[0:1], 3), (rate, vec.at[1:2], 3), (skip, vec.at[2:3], 3), (k_inner, kern.at[:, 0:CH], 4),
-        (k_state, kern.at[:, CH:CONV], 4), (gain, gain_v, 5), (w_gate, wg, 6), (w_out, wo, 7),
-    )
-    for src, dst, i in copies:
-        pltpu.make_async_copy(src, dst, loc_sem.at[i]).start()
-
-    def loaded(ref, i):
-        pltpu.make_async_copy(ref, ref, loc_sem.at[i]).wait()
-
     barrier = pltpu.get_barrier_semaphore()
     for k in range(1, 8):
         pl.semaphore_signal(barrier, inc=1, device_id={"tp": (tp + k) % 8}, device_id_type=MESH)
@@ -106,44 +95,54 @@
     for s in (nxt, prv):
         pl.semaphore_signal(barrier, inc=1, device_id={"seq": s}, device_id_type=MESH)
 
+    copies = (
+        (tok, tok_t, 0), (w_inner, wall.at[:, 0:CH], 1), (w_state, wall.at[:, CH:CONV], 1), (w_step, step_t, 2),
+        (bias, vec.at[0:1], 3), (rate, vec.at[1:2], 3), (skip, vec.at[2:3], 3), (k_inner, kern.at[:, 0:CH], 4),
+        (k_state, kern.at[:, CH:CONV], 4), (gain, gain_v, 5), (w_gate, wg, 6), (w_out, wo, 7),
+    )
+    for src, dst, i in copies:
+        pltpu.make_async_copy(src, dst, loc_sem.at[i]).start()
+
+    def loaded(ref, i):
+        pltpu.make_async_copy(ref, ref, loc_sem.at[i]).wait()
+
+    def expanded(v):
+        hi, lo = split2(v)
+        return dot(hi, expand[...]) + dot(lo, expand[...])
+
+    phase("turn")
+    loaded(tok_t, 0)
+    xb[tp] = tok_t[...].T
+    phase("barrier")
+    pl.semaphore_wait(barrier, 19)
+
+    phase("send")
+    def piece(src, q, to, sem):
+        start, rows = PIECES[q]
+        part = xb.at[src, pl.ds(start, rows), :]
+        return remote(part, part, g_send.at[0], sem, tp=to)
+
+    def send(src, q, to, origin):
+        piece(src, q, to, g_pair.at[origin, int(q in (2, 3, 5))] if to is partner else g_near.at[origin, q]).start()
+
+    def arrived(src, q, origin):
+        piece(src, q, partner, g_near.at[origin, q]).wait_recv()
+
+    def pair_arrived(src, rows, origin):
+        part = xb.at[src, pl.ds(rows[0], rows[1]), :]
+        remote(part, part, g_send.at[0], g_pair.at[origin, 1 if rows[0] else 0], tp=partner).wait_recv()
+
+    for q in (5, 4):
+        send(tp, q, right, 0)
+        send(tp, q, left, 1)
+    for q in (5, 4):
+        send(tp, q, partner, 3)
+    phase("step_turn")
     er = lax.broadcasted_iota(jnp.int32, (ST, CH), 0)
     ec = lax.broadcasted_iota(jnp.int32, (ST, CH), 1)
     off = ec - er * 64
     expand[...] = jnp.where((off >= 0) & (off < 64), 1.0, 0.0).astype(BF16)
     small[...] = jnp.zeros_like(small)
-
-    def expanded(v):
-        hi, lo = split2(v)
-        return dot(hi, expand[...]) + dot(lo, expand[...])
-
-    phase("turn")
-    loaded(tok_t, 0)
-    xb[tp] = tok_t[...].T
-    phase("barrier")
-    pl.semaphore_wait(barrier, 19)
-
-    phase("send")
-    def piece(src, q, to, sem):
-        start, rows = PIECES[q]
-        part = xb.at[src, pl.ds(start, rows), :]
-        return remote(part, part, g_send.at[0], sem, tp=to)
-
-    def send(src, q, to, origin):
-        piece(src, q, to, g_pair.at[origin, int(q in (2, 3, 5))] if to is partner else g_near.at[origin, q]).start()
-
-    def arrived(src, q, origin):
-        piece(src, q, partner, g_near.at[origin, q]).wait_recv()
-
-    def pair_arrived(src, rows, origin):
-        part = xb.at[src, pl.ds(rows[0], rows[1]), :]
-        remote(part, part, g_send.at[0], g_pair.at[origin, 1 if rows[0] else 0], tp=partner).wait_recv()
-
-    for a, b in ((2, 3), (3, 2), (4, 4)):
-        send(tp, a, right, 0)
-        send(tp, b, left, 1)
-    for q in (5, 4):
-        send(tp, q, partner, 3)
-    phase("step_turn")
     loaded(step_t, 2)
     step_f[...] = jnp.zeros_like(step_f)
     step_f[0:HD, :] = step_t[...].astype(F32)
@@ -168,17 +167,12 @@
     pair_arrived(partner, late, 3)
     accumulate(partner, *late)
     phase("near0")
-    arrived(left, 2, 0)
+    arrived(left, 5, 0)
     send(left, 2, right, 2)
-    send(left, 2, partner, 0)
-    arrived(right, 3, 1)
+    send(left, 5, partner, 0)
+    arrived(right, 5, 1)
     send(right, 3, left, 2)
-    send(right, 3, partner, 1)
-    phase("near1")
-    arrived(left, 3, 0)
-    send(left, 3, partner, 0)
-    arrived(right, 2, 1)
-    send(right, 2, partner, 1)
+    send(right, 5, partner, 1)
     phase("near_early")
     accumulate(left, *early)
     accumulate(right, *early)
@@ -579,7 +573,7 @@
         vm((4, NQ, 64, QC), F32), vm((4, NQ, 64, QC), BF16), vm((4, NQ, 64, QC), BF16),
         vm((2, NQ, 64, QC), BF16), vm((NQ, 64, QC), BF16), vm((NQ, 64, QC), BF16),
         vm((2, 64, D // 2), BF16), vm((2, 64, D // 2), BF16), vm((128, 128), F32),
-        dma((8,)), dma((1,)), dma((3, 5)), dma((4, 2)), dma((2,)), dma((2,)), dma((2,)), dma((2,)), dma((2,)), dma((2,)),
+        dma((8,)), dma((1,)), dma((3, 6)), dma((4, 2)), dma((2,)), dma((2,)), dma((2,)), dma((2,)), dma((2,)), dma((2,)),
         dma((2,)), dma((1,)), dma((9,)), dma((1,)), dma((2 * NQ + 2,)),
     ]
     hbm = pl.BlockSpec(memory_space=pl.ANY)

time: 61.7 us -> 61.7 us (level)
  no operation moved by 1% of the time
where the time goes in v5:
time: 61.7 us; the launch traced here: 61.6 us
  Pallas kernels  60.8 us (99%)
  local copies, waits for them, and re-layouts  0.73 us (1%)
    pallas_call x1, Pallas kernels, on_device(): pl.pallas_call(kernel, name='layer', out_shape=pltpu.VMEM((ROWS // 8, D),...  60.8 us

profile of v5, /device:TPU:1, one launch (start us, length us, event | category | flops | bytes accessed | tf_op | source)
XLA Modules:
  0.0 61.6 jit_solution(6546056716748317454)
XLA Ops:
  0.0 60.8 %layer.1 = bf16[64,2560]{1,0:T(8,128)(2,1)S(1)} custom-call(bf16[320,512]{1,0:T(8,128)(2,1)} %bitcast.5, bf16[2560,640]{1,0:T(8,128)(2,1)} %w_gate.1, bf16[2560,640]{1,0:T(8,128)(2,1)} %w_inner.1, bf16[2560,256]{1,0:T(8,128)(2,1)} %w_state.1, bf16[10,2560]{1,0:T(8,128)(2,1)} %bitcast.6, f32[4,640]{1,0:T(4,128)} %k_inner.1, f32[4,256]{1,0:T(4,128)} %k_state.1, ...), custom_call_target="tpu_custom_call" | custom-call | tf_op jit(solution)/shard_map/layer/pallas_call | solution.py:581
  60.9 0.7 %copy.14 = bf16[64,2560]{1,0:T(8,128)(2,1)} copy(bf16[64,2560]{1,0:T(8,128)(2,1)S(1)} %layer.1) | data formatting | bytes 655360
